TPU v7x, 8 devices: a whole 2x2x1 slice. The times are simulated.
8 devices in a mesh: sys: 1 (over z), aux: 2 (over y), orb: 4 (over x, core).
Axes of the slice: x: 2, y: 2, z: 1, core: 2. Of those that a mesh axis runs over, the one named last changes fastest.
Arguments:
- b_tensor: float32 [768, 256, 256], P(('sys', 'aux'), 'orb')
- c_alpha: float32 [256, 20], P('sys')
- c_beta: float32 [256, 19], P('sys')
Outputs:
- output 1: float32 [256, 256], P(('sys', 'orb'), 'aux')
- output 2: float32 [256, 256], P(('sys', 'orb'), 'aux')
All inputs are finite; a program needn't handle non-finite values.
Results may differ from a plain program's by a relative error of at most 0.001.
Values are sent between devices in bfloat16 or wider.
A program may use at most 1 GiB of HBM per device.

v0:
```python
import jax
import jax.numpy as jnp
from jax import lax
from jax.sharding import PartitionSpec as P

TOP_PRECISION = lax.Precision.HIGHEST


def solution(mesh):
    orb_count = mesh.shape['orb']
    shift_pairs = [(source, (source + 1) % orb_count) for source in range(orb_count)]

    def pair_product(left, right):
        return jnp.einsum('qmi,qni->mn', left, right, precision=TOP_PRECISION, preferred_element_type=jnp.float32)

    def local_build(b_local, c_alpha, c_beta):
        m_loc = b_local.shape[1]
        n_bas = b_local.shape[2]
        orb_index = lax.axis_index('orb')
        row_start = orb_index * m_loc
        alpha_rows = lax.dynamic_slice_in_dim(c_alpha, row_start, m_loc, 0)
        beta_rows = lax.dynamic_slice_in_dim(c_beta, row_start, m_loc, 0)
        dens_rows = jnp.einsum('mi,si->ms', alpha_rows, c_alpha, precision=TOP_PRECISION, preferred_element_type=jnp.float32) + jnp.einsum('mi,si->ms', beta_rows, c_beta, precision=TOP_PRECISION, preferred_element_type=jnp.float32)
        gamma_part = jnp.einsum('qms,ms->q', b_local, dens_rows, precision=TOP_PRECISION, preferred_element_type=jnp.float32)
        gamma_vec = lax.psum(gamma_part, 'orb')
        coul_part = jnp.einsum('qmn,q->mn', b_local, gamma_vec, precision=TOP_PRECISION, preferred_element_type=jnp.float32)
        half_alpha = jnp.einsum('qml,li->qmi', b_local, c_alpha, precision=TOP_PRECISION, preferred_element_type=jnp.float32)
        half_beta = jnp.einsum('qml,li->qmi', b_local, c_beta, precision=TOP_PRECISION, preferred_element_type=jnp.float32)
        empty_rows = jnp.zeros((m_loc, n_bas), jnp.float32)
        exch_alpha = lax.dynamic_update_slice_in_dim(empty_rows, pair_product(half_alpha, half_alpha), row_start, 1)
        exch_beta = lax.dynamic_update_slice_in_dim(empty_rows, pair_product(half_beta, half_beta), row_start, 1)

        def pass_step(step, carry):
            visit_alpha, visit_beta, acc_alpha, acc_beta = carry
            visit_alpha = lax.ppermute(visit_alpha, 'orb', shift_pairs)
            visit_beta = lax.ppermute(visit_beta, 'orb', shift_pairs)
            col_start = ((orb_index - step) % orb_count) * m_loc
            acc_alpha = lax.dynamic_update_slice_in_dim(acc_alpha, pair_product(half_alpha, visit_alpha), col_start, 1)
            acc_beta = lax.dynamic_update_slice_in_dim(acc_beta, pair_product(half_beta, visit_beta), col_start, 1)
            return visit_alpha, visit_beta, acc_alpha, acc_beta

        loop_out = lax.fori_loop(1, orb_count, pass_step, (half_alpha, half_beta, exch_alpha, exch_beta))
        g_alpha = lax.psum_scatter(coul_part - loop_out[2], 'aux', scatter_dimension=1, tiled=True)
        g_beta = lax.psum_scatter(coul_part - loop_out[3], 'aux', scatter_dimension=1, tiled=True)
        return g_alpha, g_beta

    spec_b = P(('sys', 'aux'), 'orb', None)
    spec_c = P('sys', None)
    spec_g = P(('sys', 'orb'), 'aux')
    return jax.shard_map(local_build, mesh=mesh, in_specs=(spec_b, spec_c, spec_c), out_specs=(spec_g, spec_g), check_vma=False)
```

profile of v0, /device:TPU:0, one launch (start us, length us, event | category | flops | bytes accessed | tf_op | source)
XLA Modules:
  0.0 356.4 jit_solution(16617594872212126385)
XLA Ops:
  7.9 33.5 %fusion.11 = f32[384,64,20]{1,2,0:T(8,128)} fusion(f32[384,64,256]{2,1,0:T(8,128)} %param.5, f32[256,20]{0,1:T(8,128)S(1)} %copy-done), kind=kOutput, calls=%fused_computation.16 | convolution fusion | flops 1509949440 | bytes 27152384 | tf_op jit(solution)/shard_map/qml,li->qmi/dot_general | solution.py:27
  41.4 5.0 %copy.11 = f32[384,64,20]{0,1,2:T(8,128)} copy(f32[384,64,20]{1,2,0:T(8,128)} %fusion.11) | data formatting | bytes 3932160 | tf_op jit(solution)/shard_map/while | solution.py:42
  46.4 3.8 %convolution_bitcast_fusion.3 = f32[64,64]{1,0:T(8,128)S(1)} fusion(f32[384,64,20]{0,1,2:T(8,128)} %copy.11), kind=kOutput, calls=%fused_computation.9 | convolution fusion | flops 377487360 | bytes 1982464 | tf_op jit(solution)/shard_map/qmi,qni->mn/dot_general | solution.py:14
  53.3 33.6 %fusion.9 = f32[384,64,19]{1,2,0:T(8,128)} fusion(f32[384,64,256]{2,1,0:T(8,128)} %param.5, f32[256,19]{0,1:T(8,128)S(1)} %copy-done.1), kind=kOutput, calls=%fused_computation.14 | convolution fusion | flops 1434451968 | bytes 27053056 | tf_op jit(solution)/shard_map/qml,li->qmi/dot_general | solution.py:28
  86.9 5.0 %copy.12 = f32[384,64,19]{0,1,2:T(8,128)} copy(f32[384,64,19]{1,2,0:T(8,128)} %fusion.9) | data formatting | bytes 3735552 | tf_op jit(solution)/shard_map/while | solution.py:42
  92.0 3.9 %convolution_bitcast_fusion.2 = f32[64,64]{1,0:T(8,128)S(1)} fusion(f32[384,64,19]{0,1,2:T(8,128)} %copy.12), kind=kOutput, calls=%fused_computation.8 | convolution fusion | flops 358612992 | bytes 1884160 | tf_op jit(solution)/shard_map/qmi,qni->mn/dot_general | solution.py:14
  99.5 39.8 %fusion.5 = f32[384]{0:T(512)S(1)} fusion(f32[384,64,256]{2,1,0:T(8,128)} %param.5, f32[64,256,1]{1,0,2:T(8,128)S(1)} %fusion.4), kind=kOutput, calls=%fused_computation.10 | convolution fusion | flops 75497472 | bytes 25232896 | tf_op jit(solution)/shard_map/qms,ms->q/dot_general | solution.py:24
  139.2 8.7 %psum.7 = f32[384]{0:T(512)S(1)} all-reduce(f32[384]{0:T(512)S(1)} %fusion.5), channel_id=1, replica_groups=mesh['sys'=1,'aux'=2,'orb'=4] {'orb'}, use_global_device_ids=true, to_apply=%region_0.0 | all-reduce | flops 384 | bytes 3072 | tf_op jit(solution)/shard_map/psum | solution.py:25
  148.0 34.9 %fusion.2 = f32[1,64,256]{2,0,1:T(1,128)S(1)} fusion(f32[384,1,1]{0,1,2:T(1,128)S(1)} %reshape.8, f32[384,64,256]{2,1,0:T(8,128)} %param.5), kind=kOutput, calls=%fused_computation.4 | convolution fusion | flops 75497472 | bytes 25232896 | tf_op jit(solution)/shard_map/qmn,q->mn/dot_general | solution.py:26
  183.8 147.4 %while.21 = (s32[]{:T(128)}, f32[384,64,20]{0,1,2:T(8,128)}, f32[384,64,19]{0,1,2:T(8,128)}, f32[64,256]{1,0:T(8,128)S(1)}, f32[64,256]{1,0:T(8,128)S(1)}, /*ind...) while((s32[]{:T(128)}, f32[384,64,20]{0,1,2:T(8,128)}, ...), condition=%wide.region_2.3_spmd, body=%wide.region_1.2_spmd.sunk | while | flops 736100352 | bytes 30769532 | solution.py:42
  184.0 22.8 %collective-permute-done.1 = f32[384,64,19]{0,1,2:T(8,128)} collective-permute-done((f32[384,64,19]{0,1,2:T(8,128)}, f32[384,64,19]{0,1,2:T(8,128)}, u32[]{:S(2)}, u32[]{:S(2)}) %collective-permute-start.1) | collective-permute-done | bytes 1867808 | tf_op jit(solution)/shard_map/while/body/eval_jaxpr/ppermute | solution.py:36
  206.8 3.9 %convolution_bitcast_fusion.7 = f32[64,64]{1,0:T(8,128)S(1)} fusion(f32[384,64,19]{0,1,2:T(8,128)} %get-tuple-element.314, f32[384,64,19]{0,1,2:T(8,128)} %collective-permute-done.1), kind=kOutput, calls=%fused_computation.clone.1 | convolution fusion | flops 358612992 | bytes 3751936 | tf_op jit(solution)/shard_map/while/body/eval_jaxpr/qmi,qni->mn/dot_general | solution.py:14
  214.1 13.8 %collective-permute-done = f32[384,64,20]{0,1,2:T(8,128)S(1)} collective-permute-done((f32[384,64,20]{0,1,2:T(8,128)}, f32[384,64,20]{0,1,2:T(8,128)S(1)}, u32[]{:S(2)}, u32[]{:S(2)}) %collective-permute-start) | collective-permute-done | bytes 1966112 | tf_op jit(solution)/shard_map/while/body/eval_jaxpr/ppermute | solution.py:35
  227.9 3.3 convolution_bitcast_fusion.6
  233.3 22.7 %collective-permute-done.1 = f32[384,64,19]{0,1,2:T(8,128)} collective-permute-done((f32[384,64,19]{0,1,2:T(8,128)}, f32[384,64,19]{0,1,2:T(8,128)}, u32[]{:S(2)}, u32[]{:S(2)}) %collective-permute-start.1) | collective-permute-done | bytes 1867808 | tf_op jit(solution)/shard_map/while/body/eval_jaxpr/ppermute | solution.py:36
  256.0 3.9 %convolution_bitcast_fusion.7 = f32[64,64]{1,0:T(8,128)S(1)} fusion(f32[384,64,19]{0,1,2:T(8,128)} %get-tuple-element.314, f32[384,64,19]{0,1,2:T(8,128)} %collective-permute-done.1), kind=kOutput, calls=%fused_computation.clone.1 | convolution fusion | flops 358612992 | bytes 3751936 | tf_op jit(solution)/shard_map/while/body/eval_jaxpr/qmi,qni->mn/dot_general | solution.py:14
  263.1 13.9 %collective-permute-done = f32[384,64,20]{0,1,2:T(8,128)S(1)} collective-permute-done((f32[384,64,20]{0,1,2:T(8,128)}, f32[384,64,20]{0,1,2:T(8,128)S(1)}, u32[]{:S(2)}, u32[]{:S(2)}) %collective-permute-start) | collective-permute-done | bytes 1966112 | tf_op jit(solution)/shard_map/while/body/eval_jaxpr/ppermute | solution.py:35
  277.0 3.3 convolution_bitcast_fusion.6
  282.4 22.5 %collective-permute-done.1 = f32[384,64,19]{0,1,2:T(8,128)} collective-permute-done((f32[384,64,19]{0,1,2:T(8,128)}, f32[384,64,19]{0,1,2:T(8,128)}, u32[]{:S(2)}, u32[]{:S(2)}) %collective-permute-start.1) | collective-permute-done | bytes 1867808 | tf_op jit(solution)/shard_map/while/body/eval_jaxpr/ppermute | solution.py:36
  304.9 3.9 %convolution_bitcast_fusion.7 = f32[64,64]{1,0:T(8,128)S(1)} fusion(f32[384,64,19]{0,1,2:T(8,128)} %get-tuple-element.314, f32[384,64,19]{0,1,2:T(8,128)} %collective-permute-done.1), kind=kOutput, calls=%fused_computation.clone.1 | convolution fusion | flops 358612992 | bytes 3751936 | tf_op jit(solution)/shard_map/while/body/eval_jaxpr/qmi,qni->mn/dot_general | solution.py:14
  312.4 13.6 %collective-permute-done = f32[384,64,20]{0,1,2:T(8,128)S(1)} collective-permute-done((f32[384,64,20]{0,1,2:T(8,128)}, f32[384,64,20]{0,1,2:T(8,128)S(1)}, u32[]{:S(2)}, u32[]{:S(2)}) %collective-permute-start) | collective-permute-done | bytes 1966112 | tf_op jit(solution)/shard_map/while/body/eval_jaxpr/ppermute | solution.py:35
  326.0 3.3 convolution_bitcast_fusion.6
  332.6 6.7 %reduce-scatter.3.cloned.1.call-done = f32[64,128]{1,0:T(8,128)} async-done(((f32[64,256]{1,0:T(8,128)}), f32[64,128]{1,0:T(8,128)}) %reduce-scatter.3.cloned.1.call-update) | async-done | bytes 32784 | tf_op jit(solution)/shard_map/reduce_scatter | solution.py:43
  339.3 10.0 %reduce-scatter.5.cloned.1.call-done = f32[64,128]{1,0:T(8,128)} async-done(((f32[64,256]{1,0:T(8,128)}), f32[64,128]{1,0:T(8,128)}) %reduce-scatter.5.cloned.1.call-update) | async-done | bytes 32784 | tf_op jit(solution)/shard_map/reduce_scatter | solution.py:44
  (36 shorter events, 26.2 us)
Async XLA Ops:
  7.2 0.7 copy-start
  7.2 332.2 %reduce-scatter.3.cloned.1.call-start = ((), (), s32[]{:S(2)}) async-start(), calls=%async_computation.2 | async-start | bytes 98304 | tf_op jit(solution)/shard_map/reduce_scatter | solution.py:43
  50.2 3.1 copy-start.1
  183.8 23.0 %collective-permute-start.1 = (f32[384,64,19]{0,1,2:T(8,128)}, f32[384,64,19]{0,1,2:T(8,128)}, u32[]{:S(2)}, u32[]{:S(2)}) collective-permute-start(f32[384,64,19]{0,1,2:T(8,128)} %get-tuple-element.295), channel_id=1, source_target_pairs={{0,1},{1,2},{2,3},{3,0},{4,5},{5,6},{6,7},{7,4}} | collective-permute-start | bytes 5603336 | tf_op jit(solution)/shard_map/while/body/eval_jaxpr/ppermute | solution.py:36
  183.8 44.1 %collective-permute-start = (f32[384,64,20]{0,1,2:T(8,128)}, f32[384,64,20]{0,1,2:T(8,128)S(1)}, u32[]{:S(2)}, u32[]{:S(2)}) collective-permute-start(f32[384,64,20]{0,1,2:T(8,128)} %get-tuple-element.294), channel_id=1, source_target_pairs={{0,1},{1,2},{2,3},{3,0},{4,5},{5,6},{6,7},{7,4}} | collective-permute-start | bytes 5898248 | tf_op jit(solution)/shard_map/while/body/eval_jaxpr/ppermute | solution.py:35
  233.0 23.0 %collective-permute-start.1 = (f32[384,64,19]{0,1,2:T(8,128)}, f32[384,64,19]{0,1,2:T(8,128)}, u32[]{:S(2)}, u32[]{:S(2)}) collective-permute-start(f32[384,64,19]{0,1,2:T(8,128)} %get-tuple-element.295), channel_id=1, source_target_pairs={{0,1},{1,2},{2,3},{3,0},{4,5},{5,6},{6,7},{7,4}} | collective-permute-start | bytes 5603336 | tf_op jit(solution)/shard_map/while/body/eval_jaxpr/ppermute | solution.py:36
  233.0 44.1 %collective-permute-start = (f32[384,64,20]{0,1,2:T(8,128)}, f32[384,64,20]{0,1,2:T(8,128)S(1)}, u32[]{:S(2)}, u32[]{:S(2)}) collective-permute-start(f32[384,64,20]{0,1,2:T(8,128)} %get-tuple-element.294), channel_id=1, source_target_pairs={{0,1},{1,2},{2,3},{3,0},{4,5},{5,6},{6,7},{7,4}} | collective-permute-start | bytes 5898248 | tf_op jit(solution)/shard_map/while/body/eval_jaxpr/ppermute | solution.py:35
  281.9 23.0 %collective-permute-start.1 = (f32[384,64,19]{0,1,2:T(8,128)}, f32[384,64,19]{0,1,2:T(8,128)}, u32[]{:S(2)}, u32[]{:S(2)}) collective-permute-start(f32[384,64,19]{0,1,2:T(8,128)} %get-tuple-element.295), channel_id=1, source_target_pairs={{0,1},{1,2},{2,3},{3,0},{4,5},{5,6},{6,7},{7,4}} | collective-permute-start | bytes 5603336 | tf_op jit(solution)/shard_map/while/body/eval_jaxpr/ppermute | solution.py:36
  281.9 44.1 %collective-permute-start = (f32[384,64,20]{0,1,2:T(8,128)}, f32[384,64,20]{0,1,2:T(8,128)S(1)}, u32[]{:S(2)}, u32[]{:S(2)}) collective-permute-start(f32[384,64,20]{0,1,2:T(8,128)} %get-tuple-element.294), channel_id=1, source_target_pairs={{0,1},{1,2},{2,3},{3,0},{4,5},{5,6},{6,7},{7,4}} | collective-permute-start | bytes 5898248 | tf_op jit(solution)/shard_map/while/body/eval_jaxpr/ppermute | solution.py:35
  331.9 17.4 %reduce-scatter.5.cloned.1.call-start = ((), (), s32[]{:S(2)}) async-start(), calls=%async_computation.3 | async-start | bytes 98304 | tf_op jit(solution)/shard_map/reduce_scatter | solution.py:44
Sparse Core Ops, SparseCore 0:
  332.0 7.2 reduce-scatter.2
  342.1 7.2 reduce-scatter.4
where the time goes:
time: 363 us; the launch traced here: 356 us
  matrix products  172 us (47%)
  waiting for transfers between devices  127 us (35%)
  local copies, waits for them, and re-layouts  33.1 us (9%)
  between operations  14.3 us (4%)
  blocking collectives  8.74 us (2%)
    ppermute x3, waiting for transfers between devices, pass_step(): visit_beta = lax.ppermute(visit_beta, 'orb', shift_pairs)  68 us
    ppermute x3, waiting for transfers between devices, pass_step(): visit_alpha = lax.ppermute(visit_alpha, 'orb', shift_pairs)  41.3 us
    dot_general x1, matrix products, local_build(): jnp.einsum('qms,ms->q', b_local, dens_rows, precision=TOP_PRECISION, pref...  39.8 us
    dot_general x1, matrix products, local_build(): jnp.einsum('qmn,q->mn', b_local, gamma_vec, precision=TOP_PRECISION, pref...  34.9 us
    dot_general x1, matrix products, local_build(): jnp.einsum('qml,li->qmi', b_local, c_beta, precision=TOP_PRECISION, prefe...  33.6 us
    dot_general x1, matrix products, local_build(): jnp.einsum('qml,li->qmi', b_local, c_alpha, precision=TOP_PRECISION, pref...  33.5 us
    dot_general x8, matrix products, pair_product(): jnp.einsum('qmi,qni->mn', left, right, precision=TOP_PRECISION, preferred...  29.2 us
    while x6, local copies, waits for them, and re-layouts  12.8 us
  transfers between devices with their start and end apart: 8, of which 8 were waited for; matrix products, arithmetic and copies ran while one was open for 6% of the time, Pallas kernels for 0%

commit v1 on v0

v1 whole, which is shorter than its diff:
```python
import jax
import jax.numpy as jnp
from jax import lax
from jax.experimental import pallas as pl
from jax.experimental.pallas import tpu as pltpu
from jax.sharding import PartitionSpec as P

TOP = lax.Precision.HIGHEST
MESH = pl.DeviceIdType.MESH
F32 = jnp.float32

NQ = 384
ROWS = 64
NB = 256
GRP = 4
QGROUPS = 24
CHUNKS = 4
CGROUPS = QGROUPS // CHUNKS
CROWS = CGROUPS * 40
BCH = CGROUPS * GRP * ROWS
TROWS = QGROUPS * 40
AHEAD = 3


def dot(a, b, dims):
    return lax.dot_general(a, b, (dims, ((), ())), precision=TOP, preferred_element_type=F32)


def kernel(b_hbm, ca_hbm, cb_hbm, ga_ref, gb_ref,
           bv, tb, cav, cbv, ct, crep, sacc, gam, grep, kd, ko, kot, gbuf, jp, jr,
           bsem, csem, rs_s, rs_r, ps_s, ps_r, gm_s, gm_r, gk_s, gk_r, j_s, j_r):
    o = lax.axis_index('orb')
    y = lax.axis_index('aux')
    x = o // 2
    c = o % 2
    par = 2 * x + (1 - c)
    far = 2 * (1 - x)

    quarter = (far + c, far + (1 - c), par, o)
    slot = (4 + c, 6, 7, c)

    def bcopy(kind, j):
        start = pl.multiple_of((quarter[kind] * CHUNKS + j) * BCH, BCH)
        return pltpu.make_async_copy(b_hbm.at[pl.ds(start, BCH)], bv.at[pl.ds(start, BCH)], bsem.at[kind, j])

    order = [(k, j) for j in range(CHUNKS) for k in (0, 1)] + [(k, j) for k in (2, 3) for j in range(CHUNKS)]
    ca_copy = pltpu.make_async_copy(ca_hbm, cav, csem.at[0])
    cb_copy = pltpu.make_async_copy(cb_hbm, cbv, csem.at[1])
    ca_copy.start()
    cb_copy.start()
    for k, j in order[:AHEAD]:
        bcopy(k, j).start()

    barrier = pltpu.get_barrier_semaphore()
    for d in range(1, 8):
        other = lax.rem(y * 4 + o + d, 8)
        pl.semaphore_signal(barrier, inc=1, device_id={'aux': other // 4, 'orb': other % 4}, device_id_type=MESH)

    ca_copy.wait()
    cb_copy.wait()

    def assemble(dst, a, b):
        at = a.T
        bt = b.T
        dst[0:16, :] = at[0:16]
        dst[16:32, :] = bt[0:16]
        dst[32:36, :] = at[16:20]
        dst[36:39, :] = bt[16:19]
        dst[39:40, :] = jnp.zeros((1, NB), F32)

    assemble(ct, cav[...], cbv[...])
    my_rows = pl.ds(pl.multiple_of(o * ROWS, ROWS), ROWS)
    own_a = cav[my_rows, :]
    own_b = cbv[my_rows, :]
    assemble(crep, jnp.concatenate([own_a] * GRP, axis=0), jnp.concatenate([own_b] * GRP, axis=0))
    sacc[96:128, :] = jnp.zeros((32, NB), F32)

    low = lax.broadcasted_iota(jnp.int32, (8, 128), 0) < 4

    def half_transform(kind, j):
        bcopy(kind, j).wait()
        first = (quarter[kind] * CHUNKS + j) * CGROUPS

        def body(h, _):
            base = pl.multiple_of((first + 2 * h) * 256, 256)
            r2 = dot(ct[...], bv[pl.ds(base, 512), :], ((1,), (1,)))
            for u in range(2):
                r = r2[:, u * 256:(u + 1) * 256]
                sacc[pl.ds(first + 2 * h + u, 1), :] = jnp.sum(r * crep[...], axis=0, keepdims=True)
                t1 = r[32:40, :128]
                t2 = r[32:40, 128:]
                row = pl.multiple_of(j * CROWS + (2 * h + u) * 40, 8)
                tb[0, slot[kind], pl.ds(row, 16), :] = r[0:16, :128]
                tb[0, slot[kind], pl.ds(row + 16, 16), :] = r[0:16, 128:]
                tb[0, slot[kind], pl.ds(row + 32, 8), :] = jnp.where(low, t1, pltpu.roll(t2, 4, 0))
                tb[1, slot[kind], pl.ds(row, 16), :] = r[16:32, :128]
                tb[1, slot[kind], pl.ds(row + 16, 16), :] = r[16:32, 128:]
                tb[1, slot[kind], pl.ds(row + 32, 8), :] = jnp.where(low, pltpu.roll(t1, 4, 0), t2)
            return 0

        lax.fori_loop(0, CGROUPS // 2, body, 0)

    def part(spin, s, j):
        return tb.at[spin, s, pl.ds(pl.multiple_of(j * CROWS, 8), CROWS)]

    def remote_send(spin, kind, j):
        return pltpu.make_async_remote_copy(
            src_ref=part(spin, slot[kind], j), dst_ref=part(spin, 2 + c, j),
            send_sem=rs_s.at[spin, kind, j], recv_sem=rs_r.at[spin, c, j],
            device_id={'orb': quarter[kind]}, device_id_type=MESH)

    def remote_recv(spin, core, j):
        return pltpu.make_async_remote_copy(
            src_ref=part(spin, 2 + core, j), dst_ref=part(spin, 2 + core, j),
            send_sem=rs_s.at[spin, 0, j], recv_sem=rs_r.at[spin, core, j],
            device_id={'orb': par}, device_id_type=MESH)

    def partner_send(spin, which, j):
        return pltpu.make_async_remote_copy(
            src_ref=part(spin, 6 + which, j), dst_ref=part(spin, (4 + c) if which == 0 else c, j),
            send_sem=ps_s.at[spin, which, j], recv_sem=ps_r.at[spin, which, j],
            device_id={'orb': par}, device_id_type=MESH)

    for n, (k, j) in enumerate(order):
        if n + AHEAD < len(order):
            bcopy(*order[n + AHEAD]).start()
        half_transform(k, j)
        if n == 0:
            pl.semaphore_wait(barrier, 7)
        if k <= 1:
            remote_send(0, k, j).start()
        if k in (1, 2):
            for spin in range(2):
                partner_send(spin, k - 1, j).start()
        if n == 2 * CHUNKS - 1:
            for jj in range(CHUNKS):
                for kk in (0, 1):
                    remote_send(1, kk, jj).start()

    e8 = (lax.broadcasted_iota(jnp.int32, (8, NB), 1) // ROWS == lax.broadcasted_iota(jnp.int32, (8, NB), 0)).astype(F32)
    gam[o] = dot(e8, sacc[...], ((1,), (1,)))

    def gamma_send(d):
        return pltpu.make_async_remote_copy(
            src_ref=gam.at[o], dst_ref=gam.at[o], send_sem=gm_s.at[d], recv_sem=gm_r.at[d],
            device_id={'orb': lax.rem(o + d, 4)}, device_id_type=MESH)

    def gamma_recv(d):
        src = lax.rem(o + 4 - d, 4)
        return pltpu.make_async_remote_copy(
            src_ref=gam.at[src], dst_ref=gam.at[src], send_sem=gm_s.at[d], recv_sem=gm_r.at[d],
            device_id={'orb': par}, device_id_type=MESH)

    for d in range(1, 4):
        gamma_send(d).start()

    left = lax.broadcasted_iota(jnp.int32, (CROWS, 128), 1) < 64

    def merged(spin, s, j):
        a = part(spin, s, j)[...]
        b = part(spin, s + 1, j)[...]
        return jnp.concatenate([jnp.where(left, a, pltpu.roll(b, 64, 1)),
                                jnp.where(left, pltpu.roll(a, 64, 1), b)], axis=0)

    def diag_part(which):
        s = (4, 0)[which]

        def body(j, acc):
            out = []
            for spin in range(2):
                pltpu.make_async_remote_copy(
                    src_ref=part(spin, 6, j), dst_ref=part(spin, (4 + 1 - c) if which == 0 else (1 - c), j),
                    send_sem=ps_s.at[spin, which, j], recv_sem=ps_r.at[spin, which, j],
                    device_id={'orb': par}, device_id_type=MESH).wait_recv()
                m = merged(spin, s, j)
                out.append(acc[spin] + dot(m, m, ((0,), (0,))))
            return tuple(out)
        return body

    zero = jnp.zeros((128, 128), F32)
    acc = lax.fori_loop(0, CHUNKS, diag_part(0), (zero, zero))
    acc = lax.fori_loop(0, CHUNKS, diag_part(1), acc)
    for spin in range(2):
        kd[spin, 0] = acc[spin][:64]
        kd[spin, 1] = acc[spin][64:]

    def block_send(src, spin, cd, xd, yd, base, sidx):
        return pltpu.make_async_remote_copy(
            src_ref=src.at[spin, cd], dst_ref=gbuf.at[spin, base + 2 * y + c],
            send_sem=gk_s.at[spin, sidx, cd], recv_sem=gk_r.at[spin, base + 2 * y + c],
            device_id={'aux': yd, 'orb': 2 * xd + cd}, device_id_type=MESH)

    def each_block(src, spin, xd, yd, base, sidx, act):
        for cd in range(2):
            mine = jnp.logical_and(jnp.logical_and(xd == x, yd == y), c == cd)

            @pl.when(jnp.logical_not(mine))
            def _():
                act(block_send(src, spin, cd, xd, yd, base, sidx))

    start = lambda copy: copy.start()
    wait_send = lambda copy: copy.wait_send()
    for spin in range(2):
        each_block(kd, spin, x, x, 0, 0, start)

    for d in range(1, 4):
        gamma_recv(d).wait_recv()
    gsum = (gam[0] + gam[1]) + (gam[2] + gam[3])
    for k in range(GRP):
        pick = (lax.broadcasted_iota(jnp.int32, (8, 128), 0) == k).astype(F32)
        grep[k] = dot(gsum, pick, ((0,), (0,)))

    def jbody(g, acc):
        for k in range(GRP):
            row = grep[k, pl.ds(g, 1), :]
            base = pl.multiple_of(g * 256 + k * ROWS, ROWS)
            acc = acc + bv[pl.ds(base, ROWS), :] * jnp.concatenate([row, row], axis=1)
        return acc

    jacc = lax.fori_loop(0, NQ // GRP, jbody, jnp.zeros((ROWS, NB), F32))
    jp[0] = jacc[:, :128]
    jp[1] = jacc[:, 128:]
    j_copy = pltpu.make_async_remote_copy(
        src_ref=jp.at[1 - y], dst_ref=jr, send_sem=j_s, recv_sem=j_r,
        device_id={'aux': 1 - y}, device_id_type=MESH)
    j_copy.start()

    for spin in range(2):
        def obody(j, acc):
            for core in range(2):
                remote_recv(spin, core, j).wait_recv()
            return acc + dot(merged(spin, 0, j), merged(spin, 2, j), ((0,), (0,)))
        block = lax.fori_loop(0, CHUNKS, obody, zero)
        ko[spin, 0] = block[:64]
        ko[spin, 1] = block[64:]
        flip = block.T
        kot[spin, 0] = flip[:64]
        kot[spin, 1] = flip[64:]
        each_block(ko, spin, x, 1 - x, 0, 1, start)
        each_block(kot, spin, 1 - x, x, 4, 2, start)

    j_copy.wait()
    jsum = jp[y] + jr[...]

    def block_recv(spin, s):
        return pltpu.make_async_remote_copy(
            src_ref=gbuf.at[spin, s], dst_ref=gbuf.at[spin, s],
            send_sem=gk_s.at[spin, 0, 0], recv_sem=gk_r.at[spin, s],
            device_id={'orb': par}, device_id_type=MESH)

    def finish(src, count):
        for spin, out in ((0, ga_ref), (1, gb_ref)):
            total = src[spin, c]
            for d in range(1, count):
                s = lax.rem(2 * y + c + d, 4) if d < 4 else d
                block_recv(spin, s).wait_recv()
                total = total + gbuf[spin, s]
            out[...] = jsum - total

    @pl.when(x == y)
    def _():
        finish(kd, 4)

    @pl.when(x != y)
    def _():
        finish(ko, 8)

    for spin in range(2):
        each_block(kd, spin, x, x, 0, 0, wait_send)
        each_block(ko, spin, x, 1 - x, 0, 1, wait_send)
        each_block(kot, spin, 1 - x, x, 4, 2, wait_send)
        for j in range(CHUNKS):
            for k in range(2):
                remote_send(spin, k, j).wait_send()
                partner_send(spin, k, j).wait_send()
    for d in range(1, 4):
        gamma_send(d).wait_send()


def solution(mesh):
    def local_build(b_local, c_alpha, c_beta):
        b_rows = b_local.reshape(NQ * ROWS, NB)
        dma = pltpu.SemaphoreType.DMA
        vmem = pltpu.VMEM
        return pl.pallas_call(
            kernel,
            out_shape=[jax.ShapeDtypeStruct((ROWS, 128), F32)] * 2,
            in_specs=[pl.BlockSpec(memory_space=pl.ANY)] * 3,
            out_specs=[pl.BlockSpec(memory_space=vmem)] * 2,
            scratch_shapes=[
                vmem((NQ * ROWS, NB), F32),
                vmem((2, 8, TROWS, 128), F32),
                vmem((NB, 20), F32), vmem((NB, 19), F32),
                vmem((40, NB), F32), vmem((40, NB), F32),
                vmem((128, NB), F32),
                vmem((4, 8, 128), F32),
                vmem((GRP, 128, 128), F32),
                vmem((2, 2, 64, 128), F32), vmem((2, 2, 64, 128), F32), vmem((2, 2, 64, 128), F32),
                vmem((2, 8, 64, 128), F32),
                vmem((2, 64, 128), F32), vmem((64, 128), F32),
                dma((4, CHUNKS)), dma((2,)),
                dma((2, 2, CHUNKS)), dma((2, 2, CHUNKS)),
                dma((2, 2, CHUNKS)), dma((2, 2, CHUNKS)),
                dma((4,)), dma((4,)),
                dma((2, 3, 2)), dma((2, 8)),
                dma, dma,
            ],
            compiler_params=pltpu.CompilerParams(
                collective_id=0, has_side_effects=True, vmem_limit_bytes=56 * 1024 * 1024),
        )(b_rows, c_alpha, c_beta)

    spec_b = P(('sys', 'aux'), 'orb', None)
    spec_c = P('sys', None)
    spec_g = P(('sys', 'orb'), 'aux')
    return jax.shard_map(local_build, mesh=mesh, in_specs=(spec_b, spec_c, spec_c), out_specs=(spec_g, spec_g), check_vma=False)
```

time: 363 us -> 68.5 us (0.19); the launches traced: 356 us -> 68.2 us
  matrix products: 172 us -> 0 us
  waiting for transfers between devices: 127 us -> 0 us
  Pallas kernels: 0 us -> 61.8 us
  local copies, waits for them, and re-layouts: 33.1 us -> 5.74 us
  between operations: 14.3 us -> 0.64 us
  blocking collectives: 8.74 us -> 0 us
    dot_general x14 -> x0, matrix products: 172 us -> none  [the longest x1 39.8 us: local_build(): jnp.einsum('qms,ms->q', b_local, dens_rows, precision=TOP_PRECISION, pref...]
    ppermute x6 -> x0, waiting for transfers between devices: 109 us -> none  [the longest x3 68 us: pass_step(): visit_beta = lax.ppermute(visit_beta, 'orb', shift_pairs)]
    pallas_call x0 -> x1, Pallas kernels: none -> 61.8 us  [local_build(): pl.pallas_call(kernel, out_shape=[jax.ShapeDtypeStruct((ROWS, 128), F32)]...]
    while x8 -> x0, local copies, waits for them, and re-layouts: 22.8 us -> none
    reduce_scatter x2 -> x0, waiting for transfers between devices: 16.7 us -> none  [the longest x1 9.99 us: local_build(): lax.psum_scatter(coul_part - loop_out[3], 'aux', scatter_dimension=1, til...]
    psum x1 -> x0, blocking collectives: 8.74 us -> none  [local_build(): gamma_vec = lax.psum(gamma_part, 'orb')]
  transfers between devices with their start and end apart: 8 -> 0, of which waited for: 8 -> 0; matrix products, arithmetic and copies ran while one was open for 6% -> 0% of each run, Pallas kernels for 0% -> 0%
where the time goes in v1:
time: 68.5 us; the launch traced here: 68.2 us
  Pallas kernels  61.8 us (90%)
  local copies, waits for them, and re-layouts  5.74 us (8%)
    pallas_call x1, Pallas kernels, local_build(): pl.pallas_call(kernel, out_shape=[jax.ShapeDtypeStruct((ROWS, 128), F32)]...  61.8 us
    unnamed x4, local copies, waits for them, and re-layouts  5.74 us

profile of v1, /device:TPU:0, one launch (start us, length us, event | category | flops | bytes accessed | tf_op | source)
XLA Modules:
  0.0 68.2 jit_solution(5822271497878228720)
XLA Ops:
  0.6 1.5 %copy.5.ca_hbm = f32[256,20]{1,0:T(8,128)} copy(f32[256,20]{0,1:T(8,128)} %param.4) | data formatting | bytes 40960 | tf_op args[1]
  2.1 1.5 %copy.6.cb_hbm = f32[256,19]{1,0:T(8,128)} copy(f32[256,19]{0,1:T(8,128)} %param.5) | data formatting | bytes 38912 | tf_op args[2]
  3.6 61.8 %shard_map.50 = (f32[64,128]{1,0:T(8,128)}, f32[64,128]{1,0:T(8,128)}) custom-call(f32[24576,256]{1,0:T(8,128)} %bitcast.1, f32[256,20]{1,0:T(8,128)} %copy.5.ca_hbm, f32[256,19]{1,0:T(8,128)} %copy.6.cb_hbm), custom_call_target="tpu_custom_call" | custom-call | tf_op jit(solution)/shard_map/pallas_call | solution.py:285
  65.4 1.4 %copy.9 = f32[64,128]{1,0:T(8,128)} copy(f32[64,128]{1,0:T(8,128)} %get-tuple-element.4) | data formatting | bytes 65536
  66.8 1.4 %copy.10 = f32[64,128]{1,0:T(8,128)} copy(f32[64,128]{1,0:T(8,128)} %get-tuple-element.5) | data formatting | bytes 65536

commit v2 on v1

v2 whole, which is shorter than its diff:
```python
import jax
import jax.numpy as jnp
from jax import lax
from jax.experimental import pallas as pl
from jax.experimental.pallas import tpu as pltpu
from jax.sharding import PartitionSpec as P

TOP = lax.Precision.HIGHEST
MESH = pl.DeviceIdType.MESH
F32 = jnp.float32

NQ = 384
ROWS = 64
NB = 256
GRP = 4
QGROUPS = 24
CHUNKS = 6
CGROUPS = QGROUPS // CHUNKS
CROWS = (CGROUPS * 40, CGROUPS * 38)
BCH = CGROUPS * GRP * ROWS
TROWS = CHUNKS * CROWS[0]
AHEAD = 4
DEPTH = 3


def dot(a, b, dims):
    return lax.dot_general(a, b, (dims, ((), ())), precision=TOP, preferred_element_type=F32)


BF16 = jnp.bfloat16
SHRINK = 1.0 - 2.0 ** -9


def split(v):
    v1 = (v * SHRINK).astype(BF16)
    rest = v - v1.astype(F32)
    v2 = rest.astype(BF16)
    return v1, v2, (rest - v2.astype(F32)).astype(BF16)


def dot16(a, b, dims):
    return lax.dot_general(a, b, (dims, ((), ())), preferred_element_type=F32)


def kernel(b_hbm, ca_hbm, cb_hbm, s_ref, jout_ref,
           bv, tb, cav, cbv, ct, cs, crep, sacc, gam, grep, kd, ko, kot, gbuf, jp, jr,
           bsem, csem, rs_s, rs_r, ps_s, ps_r, gm_s, gm_r, gk_s, gk_r, j_s, j_r):
    o = lax.axis_index('orb')
    y = lax.axis_index('aux')
    x = o // 2
    c = o % 2
    par = 2 * x + (1 - c)
    far = 2 * (1 - x)

    quarter = (far + c, far + (1 - c), par, o)
    slot = (4 + c, 6, 7, c)

    def bcopy(kind, j):
        start = pl.multiple_of((quarter[kind] * CHUNKS + j) * BCH, BCH)
        return pltpu.make_async_copy(b_hbm.at[pl.ds(start, BCH)], bv.at[pl.ds(start, BCH)], bsem.at[kind, j])

    order = [(k, j) for j in range(CHUNKS) for k in (0, 1)] + [(k, j) for k in (2, 3) for j in range(CHUNKS)]
    ca_copy = pltpu.make_async_copy(ca_hbm, cav, csem.at[0])
    cb_copy = pltpu.make_async_copy(cb_hbm, cbv, csem.at[1])
    ca_copy.start()
    cb_copy.start()
    for k, j in order[:AHEAD]:
        bcopy(k, j).start()

    barrier = pltpu.get_barrier_semaphore()
    for d in range(1, 8):
        other = lax.rem(y * 4 + o + d, 8)
        pl.semaphore_signal(barrier, inc=1, device_id={'aux': other // 4, 'orb': other % 4}, device_id_type=MESH)

    ca_copy.wait()
    cb_copy.wait()
    ct[0:16, :] = cav[0:16, :]
    ct[16:32, :] = cbv[0:16, :]
    ct[32:36, :] = cav[16:20, :]
    ct[36:39, :] = cbv[16:19, :]
    ct[39:40, :] = jnp.zeros((1, NB), F32)
    cs[...] = jnp.concatenate([t.astype(F32) for t in split(ct[...])], axis=0).astype(BF16)
    own = ct[:, pl.ds(pl.multiple_of(x * 128, 128), 128)]
    turned = pltpu.roll(own, 64, 1)
    low = lax.broadcasted_iota(jnp.int32, (40, 128), 1) < 64
    own = jnp.where(low, jnp.where(c == 0, own, turned), jnp.where(c == 0, turned, own))
    crep[:, :128] = own
    crep[:, 128:] = own
    sacc[96:128, :] = jnp.zeros((32, NB), F32)

    def part(spin, s, j):
        return tb.at[spin, s, pl.ds(pl.multiple_of(j * CROWS[spin], 8), CROWS[spin])]

    def half_transform(kind, j):
        bcopy(kind, j).wait()
        first = (quarter[kind] * CHUNKS + j) * CGROUPS
        to_a = part(0, slot[kind], j)
        to_b = part(1, slot[kind], j)
        for h in range(CGROUPS // 2):
            base = pl.multiple_of((first + 2 * h) * 256, 256)
            b1, b2, b3 = split(bv[pl.ds(base, 512), :])
            r1 = dot16(cs[...], b1, ((1,), (1,)))
            r2 = dot16(cs[0:80, :], b2, ((1,), (1,)))
            r3 = dot16(cs[0:40, :], b3, ((1,), (1,)))
            r2 = ((r3 + r2[40:80] + r1[80:120]) + (r2[0:40] + r1[40:80])) + r1[0:40]
            for u in range(4):
                p = 4 * h + u
                r = r2[:, u * 128:(u + 1) * 128]
                to_a[16 * p:16 * p + 16, :] = r[0:16]
                to_b[16 * p:16 * p + 16, :] = r[16:32]
                to_a[128 + 4 * p:132 + 4 * p, :] = r[32:36]
                to_b[128 + 3 * p:131 + 3 * p, :] = r[36:39]
            for u in range(2):
                r = r2[:, u * 256:(u + 1) * 256]
                sacc[pl.ds(first + 2 * h + u, 1), :] = jnp.sum(r * crep[...], axis=0, keepdims=True)

    def remote_send(spin, kind, j):
        return pltpu.make_async_remote_copy(
            src_ref=part(spin, slot[kind], j), dst_ref=part(spin, 2 + c, j),
            send_sem=rs_s.at[spin, kind, j], recv_sem=rs_r.at[spin, c, j],
            device_id={'orb': quarter[kind]}, device_id_type=MESH)

    def remote_recv(spin, core, j):
        return pltpu.make_async_remote_copy(
            src_ref=part(spin, 2 + core, j), dst_ref=part(spin, 2 + core, j),
            send_sem=rs_s.at[spin, 0, j], recv_sem=rs_r.at[spin, core, j],
            device_id={'orb': par}, device_id_type=MESH)

    def partner_send(spin, which, j):
        return pltpu.make_async_remote_copy(
            src_ref=part(spin, 6 + which, j), dst_ref=part(spin, (4 + c) if which == 0 else c, j),
            send_sem=ps_s.at[spin, which, j], recv_sem=ps_r.at[spin, which, j],
            device_id={'orb': par}, device_id_type=MESH)

    def partner_recv(spin, which, j):
        return pltpu.make_async_remote_copy(
            src_ref=part(spin, 6, j), dst_ref=part(spin, (5 - c) if which == 0 else (1 - c), j),
            send_sem=ps_s.at[spin, which, j], recv_sem=ps_r.at[spin, which, j],
            device_id={'orb': par}, device_id_type=MESH)

    items = [(spin, k, j) for spin in range(2) for k, j in order[:2 * CHUNKS]]
    issued = [0]

    def issue(upto):
        while issued[0] < min(upto, len(items)):
            n = issued[0]
            if n >= 2 * CHUNKS:
                remote_send(*items[n - DEPTH]).wait_send()
            remote_send(*items[n]).start()
            issued[0] = n + 1

    half_transform(0, 0)
    for k, j in order[AHEAD:]:
        bcopy(k, j).start()
    pl.semaphore_wait(barrier, 7)
    issue(1)
    half_transform(1, 0)
    issue(2)
    issued[0] = 2 * CHUNKS

    def pair(j, _):
        for k in (0, 1):
            half_transform(k, j)
            remote_send(0, k, j).start()
        return 0

    lax.fori_loop(1, CHUNKS, pair, 0)

    def back(j, _):
        for spin in range(2):
            partner_send(spin, 0, j).start()
        half_transform(2, j)
        for spin in range(2):
            partner_send(spin, 1, j).start()
        return 0

    lax.fori_loop(0, CHUNKS, back, 0)

    def home(j, _):
        half_transform(3, j)
        return 0

    lax.fori_loop(0, CHUNKS - 2, home, 0)
    issue(2 * CHUNKS + 1)
    lax.fori_loop(CHUNKS - 2, CHUNKS, home, 0)
    issue(2 * CHUNKS + 2)

    e8 = (lax.broadcasted_iota(jnp.int32, (8, NB), 1) // ROWS == lax.broadcasted_iota(jnp.int32, (8, NB), 0)).astype(F32)
    gam[o] = dot(e8, sacc[...], ((1,), (1,)))

    def gamma_send(d):
        return pltpu.make_async_remote_copy(
            src_ref=gam.at[o], dst_ref=gam.at[o], send_sem=gm_s.at[d], recv_sem=gm_r.at[d],
            device_id={'orb': lax.rem(o + d, 4)}, device_id_type=MESH)

    def gamma_recv(d):
        src = lax.rem(o + 4 - d, 4)
        return pltpu.make_async_remote_copy(
            src_ref=gam.at[src], dst_ref=gam.at[src], send_sem=gm_s.at[d], recv_sem=gm_r.at[d],
            device_id={'orb': par}, device_id_type=MESH)

    for d in range(1, 4):
        gamma_send(d).start()

    def merged(spin, s, j, count=1):
        rows = count * CROWS[spin]
        at = pl.ds(pl.multiple_of(j * CROWS[spin], 8), rows)
        a = tb[spin, s, at]
        b = tb[spin, s + 1, at]
        left = lax.broadcasted_iota(jnp.int32, (rows, 128), 1) < 64
        return jnp.concatenate([jnp.where(left, a, pltpu.roll(b, 64, 1)),
                                jnp.where(left, pltpu.roll(a, 64, 1), b)], axis=0)

    zero = jnp.zeros((128, 128), F32)
    half = CHUNKS // 2
    for spin in range(2):
        acc = zero
        for which in range(2):
            def dbody(h, acc):
                for u in range(half):
                    partner_recv(spin, which, h * half + u).wait_recv()
                m = merged(spin, (4, 0)[which], h * half, half)
                return acc + dot(m, m, ((0,), (0,)))
            acc = lax.fori_loop(0, 2, dbody, acc)
            issue(issued[0] + 1)
        kd[spin, 0] = acc[:64]
        kd[spin, 1] = acc[64:]

    def block_send(src, spin, cd, xd, yd, base, sidx):
        return pltpu.make_async_remote_copy(
            src_ref=src.at[spin, cd], dst_ref=gbuf.at[spin, base + 2 * y + c],
            send_sem=gk_s.at[spin, sidx, cd], recv_sem=gk_r.at[spin, base + 2 * y + c],
            device_id={'aux': yd, 'orb': 2 * xd + cd}, device_id_type=MESH)

    def each_block(src, spin, xd, yd, base, sidx, act):
        for cd in range(2):
            mine = jnp.logical_and(jnp.logical_and(xd == x, yd == y), c == cd)

            @pl.when(jnp.logical_not(mine))
            def _():
                act(block_send(src, spin, cd, xd, yd, base, sidx))

    start = lambda copy: copy.start()
    wait_send = lambda copy: copy.wait_send()
    for spin in range(2):
        each_block(kd, spin, x, x, 0, 0, start)

    for d in range(1, 4):
        gamma_recv(d).wait_recv()
    gsum = (gam[0] + gam[1]) + (gam[2] + gam[3])
    for k in range(GRP):
        pick = (lax.broadcasted_iota(jnp.int32, (8, 128), 0) == k).astype(F32)
        grep[k] = dot(gsum, pick, ((0,), (0,)))

    def jbody(g, acc):
        for k in range(GRP):
            row = grep[k, pl.ds(g, 1), :]
            base = pl.multiple_of(g * 256 + k * ROWS, ROWS)
            acc = acc + bv[pl.ds(base, ROWS), :] * jnp.concatenate([row, row], axis=1)
        return acc

    jacc = lax.fori_loop(0, NQ // GRP, jbody, jnp.zeros((ROWS, NB), F32))
    jp[0] = jacc[:, :128]
    jp[1] = jacc[:, 128:]
    j_copy = pltpu.make_async_remote_copy(
        src_ref=jp.at[1 - y], dst_ref=jr, send_sem=j_s, recv_sem=j_r,
        device_id={'aux': 1 - y}, device_id_type=MESH)
    j_copy.start()
    issue(issued[0] + 1)

    def block_recv(spin, s):
        return pltpu.make_async_remote_copy(
            src_ref=gbuf.at[spin, s], dst_ref=gbuf.at[spin, s],
            send_sem=gk_s.at[spin, 0, 0], recv_sem=gk_r.at[spin, s],
            device_id={'orb': par}, device_id_type=MESH)

    def finish(spin, src, count):
        total = src[spin, c]
        for d in range(1, count):
            s = lax.rem(2 * y + c + d, 4) if d < 4 else d
            block_recv(spin, s).wait_recv()
            total = total + gbuf[spin, s]
        s_ref[spin * 64:spin * 64 + 64, :] = total

    for spin in range(2):
        block = zero
        for j in range(CHUNKS):
            if spin == 1:
                issue(2 * CHUNKS + 2 * j + 1 + DEPTH)
            for core in range(2):
                remote_recv(spin, core, j).wait_recv()
            block = block + dot(merged(spin, 0, j), merged(spin, 2, j), ((0,), (0,)))
        ko[spin, 0] = block[:64]
        ko[spin, 1] = block[64:]
        flip = block.T
        kot[spin, 0] = flip[:64]
        kot[spin, 1] = flip[64:]
        each_block(ko, spin, x, 1 - x, 0, 1, start)
        each_block(kot, spin, 1 - x, x, 4, 2, start)

    j_copy.wait()
    jout_ref[...] = jp[y] + jr[...]

    @pl.when(x == y)
    def _():
        finish(0, kd, 4)
        finish(1, kd, 4)

    @pl.when(x != y)
    def _():
        finish(0, ko, 8)
        finish(1, ko, 8)

    for spin in range(2):
        each_block(kd, spin, x, x, 0, 0, wait_send)
        each_block(ko, spin, x, 1 - x, 0, 1, wait_send)
        each_block(kot, spin, 1 - x, x, 4, 2, wait_send)
        for j in range(CHUNKS):
            for k in range(2):
                partner_send(spin, k, j).wait_send()
    waited = len(items) - DEPTH
    for n, item in enumerate(items):
        if n < 2 * CHUNKS - DEPTH or n >= waited:
            remote_send(*item).wait_send()
    for d in range(1, 4):
        gamma_send(d).wait_send()


def solution(mesh):
    def local_build(b_local, c_alpha, c_beta):
        b_rows = b_local.reshape(NQ * ROWS, NB)
        dma = pltpu.SemaphoreType.DMA
        vmem = pltpu.VMEM
        neg, coul = pl.pallas_call(
            kernel,
            out_shape=[jax.ShapeDtypeStruct((2 * ROWS, 128), F32), jax.ShapeDtypeStruct((ROWS, 128), F32)],
            in_specs=[pl.BlockSpec(memory_space=pl.ANY)] * 3,
            out_specs=[pl.BlockSpec(memory_space=vmem)] * 2,
            scratch_shapes=[
                vmem((NQ * ROWS, NB), F32),
                vmem((2, 8, TROWS, 128), F32),
                vmem((20, NB), F32), vmem((19, NB), F32),
                vmem((40, NB), F32), vmem((120, NB), BF16), vmem((40, NB), F32),
                vmem((128, NB), F32),
                vmem((4, 8, 128), F32),
                vmem((GRP, 128, 128), F32),
                vmem((2, 2, 64, 128), F32), vmem((2, 2, 64, 128), F32), vmem((2, 2, 64, 128), F32),
                vmem((2, 8, 64, 128), F32),
                vmem((2, 64, 128), F32), vmem((64, 128), F32),
                dma((4, CHUNKS)), dma((2,)),
                dma((2, 2, CHUNKS)), dma((2, 2, CHUNKS)),
                dma((2, 2, CHUNKS)), dma((2, 2, CHUNKS)),
                dma((4,)), dma((4,)),
                dma((2, 3, 2)), dma((2, 8)),
                dma, dma,
            ],
            compiler_params=pltpu.CompilerParams(
                collective_id=0, has_side_effects=True, vmem_limit_bytes=56 * 1024 * 1024),
        )(b_rows, c_alpha.T, c_beta.T)
        return coul - neg[:ROWS], coul - neg[ROWS:]

    spec_b = P(('sys', 'aux'), 'orb', None)
    spec_c = P('sys', None)
    spec_g = P(('sys', 'orb'), 'aux')
    return jax.shard_map(local_build, mesh=mesh, in_specs=(spec_b, spec_c, spec_c), out_specs=(spec_g, spec_g), check_vma=False)
```

time: 68.5 us -> 56.4 us (0.82)
  Pallas kernels: 61.8 us -> 54.2 us
  local copies, waits for them, and re-layouts: 5.74 us -> 0 us
  other arithmetic: 0 us -> 1.42 us
    pallas_call x1, Pallas kernels: 61.8 us -> 54.2 us  [local_build(): pl.pallas_call(kernel, out_shape=[jax.ShapeDtypeStruct((2 * ROWS, 128), F...]
    unnamed x4 -> x0, local copies, waits for them, and re-layouts: 5.74 us -> none
    sub x0 -> x1, other arithmetic: none -> 1.42 us  [local_build(): return (coul - neg[:ROWS], coul - neg[ROWS:])]
where the time goes in v2:
time: 56.4 us; the launch traced here: 56.3 us
  Pallas kernels  54.2 us (96%)
  other arithmetic  1.42 us (3%)
  between operations  0.64 us (1%)
    pallas_call x1, Pallas kernels, local_build(): pl.pallas_call(kernel, out_shape=[jax.ShapeDtypeStruct((2 * ROWS, 128), F...  54.2 us
    sub x1, other arithmetic, local_build(): return (coul - neg[:ROWS], coul - neg[ROWS:])  1.42 us

profile of v2, /device:TPU:0, one launch (start us, length us, event | category | flops | bytes accessed | tf_op | source)
XLA Modules:
  0.0 56.3 jit_solution(4514489121315329294)
XLA Ops:
  0.6 54.2 %shard_map.50 = (f32[128,128]{1,0:T(8,128)}, f32[64,128]{1,0:T(8,128)}) custom-call(f32[24576,256]{1,0:T(8,128)} %bitcast.3, f32[20,256]{1,0:T(8,128)} %bitcast.4, f32[19,256]{1,0:T(8,128)} %bitcast.5), custom_call_target="tpu_custom_call" | custom-call | tf_op jit(solution)/shard_map/pallas_call | solution.py:334
  54.9 1.4 %slice_subtract_fusion = (f32[64,128]{1,0:T(8,128)}, f32[64,128]{1,0:T(8,128)}) fusion(f32[64,128]{1,0:T(8,128)} %get-tuple-element.4, f32[128,128]{1,0:T(8,128)} %get-tuple-element.5), kind=kLoop, calls=%fused_computation | loop fusion | flops 16384 | bytes 163840 | tf_op jit(solution)/shard_map/sub | solution.py:360

commit v3 on v2

--- a/solution.py
+++ b/solution.py
@@ -333,7 +333,7 @@
         vmem = pltpu.VMEM
         neg, coul = pl.pallas_call(
             kernel,
-            out_shape=[jax.ShapeDtypeStruct((2 * ROWS, 128), F32), jax.ShapeDtypeStruct((ROWS, 128), F32)],
+            out_shape=[pltpu.VMEM((2 * ROWS, 128), F32), pltpu.VMEM((ROWS, 128), F32)],
             in_specs=[pl.BlockSpec(memory_space=pl.ANY)] * 3,
             out_specs=[pl.BlockSpec(memory_space=vmem)] * 2,
             scratch_shapes=[

time: 56.4 us -> 55 us (0.975)
  other arithmetic: 1.42 us -> 0.63 us
  Pallas kernels: 54.2 us -> 53.6 us
    sub x1, other arithmetic: 1.42 us -> 0.63 us  [local_build(): return (coul - neg[:ROWS], coul - neg[ROWS:])]
    pallas_call x1, Pallas kernels: 54.2 us -> 53.6 us  [local_build(): pl.pallas_call(kernel, out_shape=[pltpu.VMEM((2 * ROWS, 128), F32), pltpu...]
where the time goes in v3:
time: 55 us; the launch traced here: 54.9 us
  Pallas kernels  53.6 us (97%)
  between operations  0.64 us (1%)
  other arithmetic  0.63 us (1%)
    pallas_call x1, Pallas kernels, local_build(): pl.pallas_call(kernel, out_shape=[pltpu.VMEM((2 * ROWS, 128), F32), pltpu...  53.6 us

profile of v3, /device:TPU:0, one launch (start us, length us, event | category | flops | bytes accessed | tf_op | source)
XLA Modules:
  0.0 54.9 jit_solution(7257040925876810572)
XLA Ops:
  0.6 53.6 %shard_map.50 = (f32[128,128]{1,0:T(8,128)S(1)}, f32[64,128]{1,0:T(8,128)S(1)}) custom-call(f32[24576,256]{1,0:T(8,128)} %bitcast.3, f32[20,256]{1,0:T(8,128)} %bitcast.4, f32[19,256]{1,0:T(8,128)} %bitcast.5), custom_call_target="tpu_custom_call" | custom-call | tf_op jit(solution)/shard_map/pallas_call | solution.py:334
  54.2 0.6 %slice_subtract_fusion = (f32[64,128]{1,0:T(8,128)}, f32[64,128]{1,0:T(8,128)}) fusion(f32[64,128]{1,0:T(8,128)S(1)} %get-tuple-element.4, f32[128,128]{1,0:T(8,128)S(1)} %get-tuple-element.5), kind=kLoop, calls=%fused_computation | loop fusion | flops 16384 | bytes 163840 | tf_op jit(solution)/shard_map/sub | solution.py:360

commit v4 on v3

--- a/solution.py
+++ b/solution.py
@@ -19,8 +19,10 @@
 CROWS = (CGROUPS * 40, CGROUPS * 38)
 BCH = CGROUPS * GRP * ROWS
 TROWS = CHUNKS * CROWS[0]
+SWITCH = 18
+IA, I0, I1, I2, IT, I3, I4, I5 = 4, 4, 4, 4, 12, 14, 16, 20
 AHEAD = 4
-DEPTH = 3
+DEPTH = 8
 
 
 def dot(a, b, dims):
@@ -43,8 +45,8 @@
 
 
 def kernel(b_hbm, ca_hbm, cb_hbm, s_ref, jout_ref,
-           bv, tb, cav, cbv, ct, cs, crep, sacc, gam, grep, kd, ko, kot, gbuf, jp, jr,
-           bsem, csem, rs_s, rs_r, ps_s, ps_r, gm_s, gm_r, gk_s, gk_r, j_s, j_r):
+           bv, tb, cav, cbv, ct, cs, crep, sacc, gam, grep, lt, lc, kd, kp, kt, kr, gd, gp, gt, gr, jp, jr,
+           bsem, csem, rs_s, rs_r, ps_s, ps_r, gm_s, gm_r, gd_s, gd_r, gp_s, gp_r, gt_s, gt_r, gr_s, gr_r, kr_s, kr_r, j_s, j_r, turn):
     o = lax.axis_index('orb')
     y = lax.axis_index('aux')
     x = o // 2
@@ -68,9 +70,19 @@
         bcopy(k, j).start()
 
     barrier = pltpu.get_barrier_semaphore()
-    for d in range(1, 8):
-        other = lax.rem(y * 4 + o + d, 8)
-        pl.semaphore_signal(barrier, inc=1, device_id={'aux': other // 4, 'orb': other % 4}, device_id_type=MESH)
+    def greet(yd, od):
+        pl.semaphore_signal(barrier, inc=1, device_id={'aux': yd, 'orb': od}, device_id_type=MESH)
+
+    greet(y, par)
+    for od in (far, far + 1):
+        greet(y, od)
+    for od in (2 * x, 2 * x + 1):
+        greet(1 - y, od)
+
+    @pl.when(x != y)
+    def _():
+        for od in (far, far + 1):
+            greet(1 - y, od)
 
     ca_copy.wait()
     cb_copy.wait()
@@ -120,12 +132,6 @@
             send_sem=rs_s.at[spin, kind, j], recv_sem=rs_r.at[spin, c, j],
             device_id={'orb': quarter[kind]}, device_id_type=MESH)
 
-    def remote_recv(spin, core, j):
-        return pltpu.make_async_remote_copy(
-            src_ref=part(spin, 2 + core, j), dst_ref=part(spin, 2 + core, j),
-            send_sem=rs_s.at[spin, 0, j], recv_sem=rs_r.at[spin, core, j],
-            device_id={'orb': par}, device_id_type=MESH)
-
     def partner_send(spin, which, j):
         return pltpu.make_async_remote_copy(
             src_ref=part(spin, 6 + which, j), dst_ref=part(spin, (4 + c) if which == 0 else c, j),
@@ -139,36 +145,53 @@
             device_id={'orb': par}, device_id_type=MESH)
 
     items = [(spin, k, j) for spin in range(2) for k, j in order[:2 * CHUNKS]]
+    turns = [(spin, k, j) for spin in range(2) for j in range(CHUNKS) for k in (1, 0)]
+    turns = turns[:-4] + sorted(turns[-4:], key=lambda item: -item[1])
     issued = [0]
 
     def issue(upto):
-        while issued[0] < min(upto, len(items)):
-            n = issued[0]
-            if n >= 2 * CHUNKS:
-                remote_send(*items[n - DEPTH]).wait_send()
-            remote_send(*items[n]).start()
-            issued[0] = n + 1
+        todo = range(issued[0], min(upto, len(turns)))
+        issued[0] = max(issued[0], min(upto, len(turns)))
+
+        @pl.when(c == 1)
+        def _():
+            for n in todo:
+                if n >= DEPTH:
+                    remote_send(*turns[n - DEPTH]).wait_send()
+                remote_send(*turns[n]).start()
 
     half_transform(0, 0)
     for k, j in order[AHEAD:]:
         bcopy(k, j).start()
-    pl.semaphore_wait(barrier, 7)
-    issue(1)
+    pl.semaphore_wait(barrier, jnp.where(x == y, 5, 7))
+
+    @pl.when(c == 0)
+    def _():
+        remote_send(0, 0, 0).start()
+
     half_transform(1, 0)
-    issue(2)
-    issued[0] = 2 * CHUNKS
+
+    @pl.when(c == 0)
+    def _():
+        remote_send(0, 1, 0).start()
 
     def pair(j, _):
         for k in (0, 1):
             half_transform(k, j)
-            remote_send(0, k, j).start()
-        return 0
-
-    lax.fori_loop(1, CHUNKS, pair, 0)
-
-    def back(j, _):
+
+            @pl.when(c == 0)
+            def _():
+                remote_send(0, k, j).start()
         for spin in range(2):
             partner_send(spin, 0, j).start()
+        return 0
+
+    for spin in range(2):
+        partner_send(spin, 0, 0).start()
+    lax.fori_loop(1, CHUNKS, pair, 0)
+    issue(IA)
+
+    def back(j, _):
         half_transform(2, j)
         for spin in range(2):
             partner_send(spin, 1, j).start()
@@ -176,14 +199,17 @@
 
     lax.fori_loop(0, CHUNKS, back, 0)
 
+    @pl.when(c == 0)
+    def _():
+        for item in items[2 * CHUNKS:]:
+            remote_send(*item).start()
+
     def home(j, _):
         half_transform(3, j)
         return 0
 
-    lax.fori_loop(0, CHUNKS - 2, home, 0)
-    issue(2 * CHUNKS + 1)
-    lax.fori_loop(CHUNKS - 2, CHUNKS, home, 0)
-    issue(2 * CHUNKS + 2)
+    lax.fori_loop(0, CHUNKS, home, 0)
+    issue(I0)
 
     e8 = (lax.broadcasted_iota(jnp.int32, (8, NB), 1) // ROWS == lax.broadcasted_iota(jnp.int32, (8, NB), 0)).astype(F32)
     gam[o] = dot(e8, sacc[...], ((1,), (1,)))
@@ -202,48 +228,153 @@
     for d in range(1, 4):
         gamma_send(d).start()
 
-    def merged(spin, s, j, count=1):
+    def sides(spin, s, j, count):
         rows = count * CROWS[spin]
         at = pl.ds(pl.multiple_of(j * CROWS[spin], 8), rows)
         a = tb[spin, s, at]
         b = tb[spin, s + 1, at]
         left = lax.broadcasted_iota(jnp.int32, (rows, 128), 1) < 64
-        return jnp.concatenate([jnp.where(left, a, pltpu.roll(b, 64, 1)),
-                                jnp.where(left, pltpu.roll(a, 64, 1), b)], axis=0)
-
-    zero = jnp.zeros((128, 128), F32)
+        return jnp.where(left, a, pltpu.roll(b, 64, 1)), jnp.where(left, pltpu.roll(a, 64, 1), b)
+
     half = CHUNKS // 2
     for spin in range(2):
-        acc = zero
+        cols = 2 * half * CROWS[spin]
+        acc = (jnp.zeros((128, 128), F32),) * 2
         for which in range(2):
             def dbody(h, acc):
                 for u in range(half):
                     partner_recv(spin, which, h * half + u).wait_recv()
-                m = merged(spin, (4, 0)[which], h * half, half)
-                return acc + dot(m, m, ((0,), (0,)))
+                m = jnp.concatenate(sides(spin, (4, 0)[which], h * half, half), axis=0)
+                m1, m2, m3 = split(m)
+                t1, t2, t3 = split(m.T)
+                r = dot16(jnp.concatenate([t1, t2], axis=0), jnp.concatenate([m1, m2], axis=1), ((1,), (0,)))
+                q = dot16(t1, m3, ((1,), (0,)))
+                if which == 1:
+                    lt[spin, h, :, 0:cols] = jnp.concatenate([t1, t2, t3], axis=0)
+                return acc[0] + ((r[128:, 128:] + (r[:128, 128:] + r[128:, :128])) + r[:128, :128]), acc[1] + q
             acc = lax.fori_loop(0, 2, dbody, acc)
-            issue(issued[0] + 1)
+        acc = acc[0] + (acc[1] + acc[1].T)
         kd[spin, 0] = acc[:64]
         kd[spin, 1] = acc[64:]
-
-    def block_send(src, spin, cd, xd, yd, base, sidx):
-        return pltpu.make_async_remote_copy(
-            src_ref=src.at[spin, cd], dst_ref=gbuf.at[spin, base + 2 * y + c],
-            send_sem=gk_s.at[spin, sidx, cd], recv_sem=gk_r.at[spin, base + 2 * y + c],
-            device_id={'aux': yd, 'orb': 2 * xd + cd}, device_id_type=MESH)
-
-    def each_block(src, spin, xd, yd, base, sidx, act):
-        for cd in range(2):
-            mine = jnp.logical_and(jnp.logical_and(xd == x, yd == y), c == cd)
-
-            @pl.when(jnp.logical_not(mine))
-            def _():
-                act(block_send(src, spin, cd, xd, yd, base, sidx))
+        if spin == 1:
+            for u in range(half):
+                lc[u, :, 0:2 * CROWS[1]] = jnp.concatenate(split(jnp.concatenate(sides(1, 0, half + u, 1), axis=0).T), axis=0)
+        issue(I1 if spin == 0 else I2)
+
+    def kd_send(spin, cd):
+        return pltpu.make_async_remote_copy(
+            src_ref=kd.at[spin, cd], dst_ref=gd.at[spin, 2 * y + c],
+            send_sem=gd_s.at[spin, cd], recv_sem=gd_r.at[spin, 2 * y + c],
+            device_id={'aux': x, 'orb': 2 * x + cd}, device_id_type=MESH)
+
+    def kp_send(spin, cs, cd):
+        return pltpu.make_async_remote_copy(
+            src_ref=kp.at[spin, cs, cd], dst_ref=gp.at[spin, cs, 2 * y + c],
+            send_sem=gp_s.at[spin, cs, cd], recv_sem=gp_r.at[spin, cs, 2 * y + c],
+            device_id={'aux': 1 - x, 'orb': 2 * x + cd}, device_id_type=MESH)
+
+    def kt_send(spin):
+        return pltpu.make_async_remote_copy(
+            src_ref=kt.at[spin, 1], dst_ref=gt.at[2 * y + c],
+            send_sem=gt_s, recv_sem=gt_r.at[2 * y + c],
+            device_id={'aux': x, 'orb': 2 * (1 - x) + 1}, device_id_type=MESH)
+
+    def gr_send(spin, cs):
+        return pltpu.make_async_remote_copy(
+            src_ref=kt.at[spin, cs], dst_ref=gr.at[spin, 2 * y + c],
+            send_sem=gr_s.at[spin, cs], recv_sem=gr_r.at[spin, 2 * y + c],
+            device_id={'aux': 0, 'orb': 2 * x + cs}, device_id_type=MESH)
+
+    def kr_send(spin, cs):
+        return pltpu.make_async_remote_copy(
+            src_ref=kr.at[spin, 0], dst_ref=kr.at[spin, 1],
+            send_sem=kr_s.at[spin], recv_sem=kr_r.at[spin],
+            device_id={'aux': x, 'orb': 2 * (1 - x) + cs}, device_id_type=MESH)
+
+    def relay(spin, cs):
+        @pl.when(jnp.logical_and(y == 0, c == cs))
+        def _():
+            total = kt[spin, cs]
+            for d in range(1, 4):
+                s = lax.rem(2 * y + c + d, 4)
+                landed(gr.at[spin, s], gr_r.at[spin, s])
+                total = total + gr[spin, s]
+            kr[spin, 0] = total
+            kr_send(spin, cs).start()
+
+    def landed(dst, sem):
+        return pltpu.make_async_remote_copy(
+            src_ref=dst, dst_ref=dst, send_sem=j_s, recv_sem=sem, device_id={'orb': par}, device_id_type=MESH).wait_recv()
 
     start = lambda copy: copy.start()
     wait_send = lambda copy: copy.wait_send()
+
+    def each_kd(spin, act):
+        for cd in range(2):
+            @pl.when(jnp.logical_not(jnp.logical_and(x == y, c == cd)))
+            def _():
+                act(kd_send(spin, cd))
+
+    def each_ko(spin, cs, act):
+        if (spin, cs) == (1, 1):
+            act(kt_send(spin))
+        else:
+            @pl.when(jnp.logical_not(jnp.logical_and(y == 0, c == cs)))
+            def _():
+                act(gr_send(spin, cs))
+        for cd in range(2):
+            @pl.when(jnp.logical_not(jnp.logical_and(x != y, c == cd)))
+            def _():
+                act(kp_send(spin, cs, cd))
+
     for spin in range(2):
-        each_block(kd, spin, x, x, 0, 0, start)
+        each_kd(spin, start)
+
+    @pl.when(c == 0)
+    def _():
+        for item in items[:SWITCH]:
+            remote_send(*item).wait_send()
+        pl.semaphore_signal(turn, inc=1, device_id={'orb': par}, device_id_type=MESH)
+
+    @pl.when(c == 1)
+    def _():
+        pl.semaphore_wait(turn, 1)
+
+    issue(IT)
+
+    def off_part(spin, cs, j, count, left_side, acc):
+        for u in range(count):
+            landed(part(spin, 2 + cs, j + u), rs_r.at[spin, cs, j + u])
+        rows = count * CROWS[spin]
+        v = tb[spin, 2 + cs, j * CROWS[spin]:j * CROWS[spin] + rows]
+        v1, v2, v3 = [t.astype(F32) for t in split(v)]
+        left = lax.broadcasted_iota(jnp.int32, (rows, 128), 1) < 64
+        none = jnp.zeros((rows, 128), F32)
+        w = jnp.concatenate([
+            jnp.concatenate([jnp.where(left, v1, pltpu.roll(v2, 64, 1)), jnp.where(left, v3, none)], axis=1),
+            jnp.concatenate([jnp.where(left, pltpu.roll(v1, 64, 1), v2), jnp.where(left, pltpu.roll(v3, 64, 1), none)], axis=1),
+        ], axis=0).astype(BF16)
+        r = dot16(left_side[:, 0:2 * rows], w, ((1,), (0,)))
+        return acc + ((r[256:] + r[128:256]) + r[:128])
+
+    def off_done(spin, cs, acc):
+        block = acc[:, :128] + acc[:, 128:]
+        block = block + pltpu.roll(block, 64, 1)
+        left = lax.broadcasted_iota(jnp.int32, (32, 128), 1) < 64
+        for cd in range(2):
+            kp[spin, cs, cd] = jnp.where(left, block[64 * cd:64 * cd + 32], pltpu.roll(block[64 * cd + 32:64 * cd + 64], 64, 1))
+        kt[spin, cs] = block.T[:64]
+        each_ko(spin, cs, start)
+
+    zero = jnp.zeros((128, NB), F32)
+    for spin in range(2):
+        acc = zero
+        for h in range(2):
+            acc = off_part(spin, 0, h * half, half, lt.at[spin, h], acc)
+        off_done(spin, 0, acc)
+        issue(I3 if spin == 0 else I4)
+        if spin == 1:
+            relay(0, 0)
 
     for d in range(1, 4):
         gamma_recv(d).wait_recv()
@@ -266,62 +397,98 @@
         src_ref=jp.at[1 - y], dst_ref=jr, send_sem=j_s, recv_sem=j_r,
         device_id={'aux': 1 - y}, device_id_type=MESH)
     j_copy.start()
-    issue(issued[0] + 1)
-
-    def block_recv(spin, s):
-        return pltpu.make_async_remote_copy(
-            src_ref=gbuf.at[spin, s], dst_ref=gbuf.at[spin, s],
-            send_sem=gk_s.at[spin, 0, 0], recv_sem=gk_r.at[spin, s],
-            device_id={'orb': par}, device_id_type=MESH)
-
-    def finish(spin, src, count):
-        total = src[spin, c]
-        for d in range(1, count):
-            s = lax.rem(2 * y + c + d, 4) if d < 4 else d
-            block_recv(spin, s).wait_recv()
-            total = total + gbuf[spin, s]
+    issue(I5)
+
+    relay(1, 0)
+
+    acc = zero
+    for h in range(2):
+        issue(2 * (h + 1) * half + DEPTH - 1)
+        acc = off_part(0, 1, h * half, half, lt.at[0, h], acc)
+    off_done(0, 1, acc)
+
+    def finish_kd(spin):
+        total = kd[spin, c]
+        for d in range(1, 4):
+            s = lax.rem(2 * y + c + d, 4)
+            landed(gd.at[spin, s], gd_r.at[spin, s])
+            total = total + gd[spin, s]
         s_ref[spin * 64:spin * 64 + 64, :] = total
 
+    def finish_ko(spin):
+        pair_sum = []
+        for cs in range(2):
+            total = kp[spin, cs, c]
+            for d in range(1, 4):
+                s = lax.rem(2 * y + c + d, 4)
+                landed(gp.at[spin, cs, s], gp_r.at[spin, cs, s])
+                total = total + gp[spin, cs, s]
+            pair_sum.append(total)
+        if spin == 0:
+            landed(kr.at[0, 1], kr_r.at[0])
+            turned = kr[0, 1]
+        else:
+            @pl.when(c == 0)
+            def _():
+                landed(kr.at[1, 1], kr_r.at[1])
+
+            @pl.when(c == 1)
+            def _():
+                for s in range(4):
+                    landed(gt.at[s], gt_r.at[s])
+                kr[1, 1] = (gt[0] + gt[1]) + (gt[2] + gt[3])
+            turned = kr[1, 1]
+        a, b = pair_sum
+        left = lax.broadcasted_iota(jnp.int32, (32, 128), 1) < 64
+        s_ref[spin * 64:spin * 64 + 32, :] = turned[:32] + jnp.where(left, a, pltpu.roll(b, 64, 1))
+        s_ref[spin * 64 + 32:spin * 64 + 64, :] = turned[32:] + jnp.where(left, pltpu.roll(a, 64, 1), b)
+
+    acc = zero
+    for j, count in ((0, half), (half, 1), (half + 1, 1), (half + 2, 1)):
+        issue(2 * (CHUNKS + j + count) + DEPTH)
+        acc = off_part(1, 1, j, count, lt.at[1, 0] if j == 0 else lc.at[j - half], acc)
+        if j == 0:
+            relay(0, 1)
+            j_copy.wait()
+            jout_ref[...] = jp[y] + jr[...]
+
+            @pl.when(x == y)
+            def _():
+                finish_kd(0)
+                finish_kd(1)
+
+            @pl.when(x != y)
+            def _():
+                finish_ko(0)
+    off_done(1, 1, acc)
+
+    @pl.when(x != y)
+    def _():
+        finish_ko(1)
+
     for spin in range(2):
-        block = zero
-        for j in range(CHUNKS):
-            if spin == 1:
-                issue(2 * CHUNKS + 2 * j + 1 + DEPTH)
-            for core in range(2):
-                remote_recv(spin, core, j).wait_recv()
-            block = block + dot(merged(spin, 0, j), merged(spin, 2, j), ((0,), (0,)))
-        ko[spin, 0] = block[:64]
-        ko[spin, 1] = block[64:]
-        flip = block.T
-        kot[spin, 0] = flip[:64]
-        kot[spin, 1] = flip[64:]
-        each_block(ko, spin, x, 1 - x, 0, 1, start)
-        each_block(kot, spin, 1 - x, x, 4, 2, start)
-
-    j_copy.wait()
-    jout_ref[...] = jp[y] + jr[...]
-
-    @pl.when(x == y)
-    def _():
-        finish(0, kd, 4)
-        finish(1, kd, 4)
-
-    @pl.when(x != y)
-    def _():
-        finish(0, ko, 8)
-        finish(1, ko, 8)
-
-    for spin in range(2):
-        each_block(kd, spin, x, x, 0, 0, wait_send)
-        each_block(ko, spin, x, 1 - x, 0, 1, wait_send)
-        each_block(kot, spin, 1 - x, x, 4, 2, wait_send)
+        each_kd(spin, wait_send)
+        for cs in range(2):
+            each_ko(spin, cs, wait_send)
         for j in range(CHUNKS):
             for k in range(2):
                 partner_send(spin, k, j).wait_send()
-    waited = len(items) - DEPTH
-    for n, item in enumerate(items):
-        if n < 2 * CHUNKS - DEPTH or n >= waited:
+
+    @pl.when(c == 0)
+    def _():
+        for item in items[SWITCH:]:
             remote_send(*item).wait_send()
+
+    @pl.when(c == 1)
+    def _():
+        for item in turns[-DEPTH:]:
+            remote_send(*item).wait_send()
+
+    for spin, cs in ((0, 0), (1, 0), (0, 1)):
+        @pl.when(jnp.logical_and(y == 0, c == cs))
+        def _():
+            kr_send(spin, cs).wait_send()
+
     for d in range(1, 4):
         gamma_send(d).wait_send()
 
@@ -344,15 +511,20 @@
                 vmem((128, NB), F32),
                 vmem((4, 8, 128), F32),
                 vmem((GRP, 128, 128), F32),
-                vmem((2, 2, 64, 128), F32), vmem((2, 2, 64, 128), F32), vmem((2, 2, 64, 128), F32),
-                vmem((2, 8, 64, 128), F32),
+                vmem((2, 2, 384, CHUNKS * CROWS[0]), BF16),
+                vmem((CHUNKS // 2, 384, 384), BF16),
+                vmem((2, 2, 64, 128), F32), vmem((2, 2, 2, 32, 128), F32), vmem((2, 2, 64, 128), F32),
+                vmem((2, 2, 64, 128), F32),
+                vmem((2, 4, 64, 128), F32), vmem((2, 2, 4, 32, 128), F32), vmem((4, 64, 128), F32),
+                vmem((2, 4, 64, 128), F32),
                 vmem((2, 64, 128), F32), vmem((64, 128), F32),
                 dma((4, CHUNKS)), dma((2,)),
                 dma((2, 2, CHUNKS)), dma((2, 2, CHUNKS)),
                 dma((2, 2, CHUNKS)), dma((2, 2, CHUNKS)),
                 dma((4,)), dma((4,)),
-                dma((2, 3, 2)), dma((2, 8)),
-                dma, dma,
+                dma((2, 2)), dma((2, 4)), dma((2, 2, 2)), dma((2, 2, 4)), dma, dma((4,)),
+                dma((2, 2)), dma((2, 4)), dma((2,)), dma((2,)),
+                dma, dma, pltpu.SemaphoreType.REGULAR,
             ],
             compiler_params=pltpu.CompilerParams(
                 collective_id=0, has_side_effects=True, vmem_limit_bytes=56 * 1024 * 1024),

time: 55 us -> 54.2 us (0.985)
  the two profiles are of different devices: /device:TPU:0 before, /device:TPU:3 now
where the time goes in v4:
time: 54.2 us; the launch traced here: 54.1 us
  Pallas kernels  52.8 us (97%)
  between operations  0.64 us (1%)
  other arithmetic  0.63 us (1%)
    pallas_call x1, Pallas kernels, local_build(): pl.pallas_call(kernel, out_shape=[pltpu.VMEM((2 * ROWS, 128), F32), pltpu...  52.8 us

profile of v4, /device:TPU:3, one launch (start us, length us, event | category | flops | bytes accessed | tf_op | source)
XLA Modules:
  0.0 54.1 jit_solution(7138860790818620765)
XLA Ops:
  0.6 52.8 %shard_map.50 = (f32[128,128]{1,0:T(8,128)S(1)}, f32[64,128]{1,0:T(8,128)S(1)}) custom-call(f32[24576,256]{1,0:T(8,128)} %bitcast.3, f32[20,256]{1,0:T(8,128)} %bitcast.4, f32[19,256]{1,0:T(8,128)} %bitcast.5), custom_call_target="tpu_custom_call" | custom-call | tf_op jit(solution)/shard_map/pallas_call | solution.py:501
  53.5 0.6 %slice_subtract_fusion = (f32[64,128]{1,0:T(8,128)}, f32[64,128]{1,0:T(8,128)}) fusion(f32[64,128]{1,0:T(8,128)S(1)} %get-tuple-element.4, f32[128,128]{1,0:T(8,128)S(1)} %get-tuple-element.5), kind=kLoop, calls=%fused_computation | loop fusion | flops 16384 | bytes 163840 | tf_op jit(solution)/shard_map/sub | solution.py:532

commit v5 on v4

--- a/solution.py
+++ b/solution.py
@@ -19,10 +19,11 @@
 CROWS = (CGROUPS * 40, CGROUPS * 38)
 BCH = CGROUPS * GRP * ROWS
 TROWS = CHUNKS * CROWS[0]
-SWITCH = 18
-IA, I0, I1, I2, IT, I3, I4, I5 = 4, 4, 4, 4, 12, 14, 16, 20
+SWITCH = 14
+LAST = ((1, 3), (0, 3), (1, 4), (1, 5), (0, 4), (0, 5))
+IA, I0, I1, I2, IT, I3, I4, I5 = 1, 1, 1, 1, 4, 4, 5, 6
 AHEAD = 4
-DEPTH = 8
+DEPTH = 6
 
 
 def dot(a, b, dims):
@@ -64,9 +65,19 @@
     order = [(k, j) for j in range(CHUNKS) for k in (0, 1)] + [(k, j) for k in (2, 3) for j in range(CHUNKS)]
     ca_copy = pltpu.make_async_copy(ca_hbm, cav, csem.at[0])
     cb_copy = pltpu.make_async_copy(cb_hbm, cbv, csem.at[1])
+    def bpiece(kind, j, u):
+        rows = BCH // 4
+        start = pl.multiple_of((quarter[kind] * CHUNKS + j) * BCH + u * rows, rows)
+        return pltpu.make_async_copy(b_hbm.at[pl.ds(start, rows)], bv.at[pl.ds(start, rows)], bsem.at[kind, j])
+
+    for u in range(4):
+        bpiece(0, 0, u).start()
     ca_copy.start()
     cb_copy.start()
-    for k, j in order[:AHEAD]:
+    for k, j in order[1:1]:
+        for u in range(4):
+            bpiece(k, j, u).start()
+    for k, j in order[1:AHEAD]:
         bcopy(k, j).start()
 
     barrier = pltpu.get_barrier_semaphore()
@@ -100,8 +111,8 @@
     crep[:, 128:] = own
     sacc[96:128, :] = jnp.zeros((32, NB), F32)
 
-    def part(spin, s, j):
-        return tb.at[spin, s, pl.ds(pl.multiple_of(j * CROWS[spin], 8), CROWS[spin])]
+    def part(spin, s, j, count=1):
+        return tb.at[spin, s, pl.ds(pl.multiple_of(j * CROWS[spin], 8), count * CROWS[spin])]
 
     def half_transform(kind, j):
         bcopy(kind, j).wait()
@@ -126,9 +137,9 @@
                 r = r2[:, u * 256:(u + 1) * 256]
                 sacc[pl.ds(first + 2 * h + u, 1), :] = jnp.sum(r * crep[...], axis=0, keepdims=True)
 
-    def remote_send(spin, kind, j):
-        return pltpu.make_async_remote_copy(
-            src_ref=part(spin, slot[kind], j), dst_ref=part(spin, 2 + c, j),
+    def remote_send(spin, kind, j, count=1):
+        return pltpu.make_async_remote_copy(
+            src_ref=part(spin, slot[kind], j, count), dst_ref=part(spin, 2 + c, j, count),
             send_sem=rs_s.at[spin, kind, j], recv_sem=rs_r.at[spin, c, j],
             device_id={'orb': quarter[kind]}, device_id_type=MESH)
 
@@ -144,9 +155,11 @@
             send_sem=ps_s.at[spin, which, j], recv_sem=ps_r.at[spin, which, j],
             device_id={'orb': par}, device_id_type=MESH)
 
-    items = [(spin, k, j) for spin in range(2) for k, j in order[:2 * CHUNKS]]
-    turns = [(spin, k, j) for spin in range(2) for j in range(CHUNKS) for k in (1, 0)]
-    turns = turns[:-4] + sorted(turns[-4:], key=lambda item: -item[1])
+    half = CHUNKS // 2
+    items = [(0, k, j, 1) for k, j in order[:2 * CHUNKS]] + [(1, k, j, half) for j in (0, half) for k in (0, 1)]
+    turns = [(0, k, j, half) for j in (0, half) for k in (1, 0)] + [(1, k, 0, half) for k in (1, 0)]
+    turns += [(1, k, j, 1) for k, j in LAST]
+    issued = [0]
     issued = [0]
 
     def issue(upto):
@@ -236,7 +249,6 @@
         left = lax.broadcasted_iota(jnp.int32, (rows, 128), 1) < 64
         return jnp.where(left, a, pltpu.roll(b, 64, 1)), jnp.where(left, pltpu.roll(a, 64, 1), b)
 
-    half = CHUNKS // 2
     for spin in range(2):
         cols = 2 * half * CROWS[spin]
         acc = (jnp.zeros((128, 128), F32),) * 2
@@ -279,11 +291,14 @@
             send_sem=gt_s, recv_sem=gt_r.at[2 * y + c],
             device_id={'aux': x, 'orb': 2 * (1 - x) + 1}, device_id_type=MESH)
 
+    def hub(spin, cs):
+        return x if (spin, cs) in ((0, 0), (1, 0)) else 0
+
     def gr_send(spin, cs):
         return pltpu.make_async_remote_copy(
             src_ref=kt.at[spin, cs], dst_ref=gr.at[spin, 2 * y + c],
             send_sem=gr_s.at[spin, cs], recv_sem=gr_r.at[spin, 2 * y + c],
-            device_id={'aux': 0, 'orb': 2 * x + cs}, device_id_type=MESH)
+            device_id={'aux': hub(spin, cs), 'orb': 2 * x + cs}, device_id_type=MESH)
 
     def kr_send(spin, cs):
         return pltpu.make_async_remote_copy(
@@ -292,7 +307,7 @@
             device_id={'aux': x, 'orb': 2 * (1 - x) + cs}, device_id_type=MESH)
 
     def relay(spin, cs):
-        @pl.when(jnp.logical_and(y == 0, c == cs))
+        @pl.when(jnp.logical_and(y == hub(spin, cs), c == cs))
         def _():
             total = kt[spin, cs]
             for d in range(1, 4):
@@ -319,7 +334,7 @@
         if (spin, cs) == (1, 1):
             act(kt_send(spin))
         else:
-            @pl.when(jnp.logical_not(jnp.logical_and(y == 0, c == cs)))
+            @pl.when(jnp.logical_not(jnp.logical_and(y == hub(spin, cs), c == cs)))
             def _():
                 act(gr_send(spin, cs))
         for cd in range(2):
@@ -343,8 +358,9 @@
     issue(IT)
 
     def off_part(spin, cs, j, count, left_side, acc):
-        for u in range(count):
-            landed(part(spin, 2 + cs, j + u), rs_r.at[spin, cs, j + u])
+        step = 1 if (spin, cs) == (0, 0) else count
+        for u in range(0, count, step):
+            landed(part(spin, 2 + cs, j + u, step), rs_r.at[spin, cs, j + u])
         rows = count * CROWS[spin]
         v = tb[spin, 2 + cs, j * CROWS[spin]:j * CROWS[spin] + rows]
         v1, v2, v3 = [t.astype(F32) for t in split(v)]
@@ -361,9 +377,9 @@
         block = acc[:, :128] + acc[:, 128:]
         block = block + pltpu.roll(block, 64, 1)
         left = lax.broadcasted_iota(jnp.int32, (32, 128), 1) < 64
+        kt[spin, cs] = block.T[:64]
         for cd in range(2):
             kp[spin, cs, cd] = jnp.where(left, block[64 * cd:64 * cd + 32], pltpu.roll(block[64 * cd + 32:64 * cd + 64], 64, 1))
-        kt[spin, cs] = block.T[:64]
         each_ko(spin, cs, start)
 
     zero = jnp.zeros((128, NB), F32)
@@ -403,7 +419,7 @@
 
     acc = zero
     for h in range(2):
-        issue(2 * (h + 1) * half + DEPTH - 1)
+        issue(6 + 2 * h)
         acc = off_part(0, 1, h * half, half, lt.at[0, h], acc)
     off_done(0, 1, acc)
 
@@ -445,9 +461,10 @@
 
     acc = zero
     for j, count in ((0, half), (half, 1), (half + 1, 1), (half + 2, 1)):
-        issue(2 * (CHUNKS + j + count) + DEPTH)
+        issue(10 if j == 0 else 12)
         acc = off_part(1, 1, j, count, lt.at[1, 0] if j == 0 else lc.at[j - half], acc)
         if j == 0:
+            issue(12)
             relay(0, 1)
             j_copy.wait()
             jout_ref[...] = jp[y] + jr[...]
@@ -485,7 +502,7 @@
             remote_send(*item).wait_send()
 
     for spin, cs in ((0, 0), (1, 0), (0, 1)):
-        @pl.when(jnp.logical_and(y == 0, c == cs))
+        @pl.when(jnp.logical_and(y == hub(spin, cs), c == cs))
         def _():
             kr_send(spin, cs).wait_send()
 

time: 54.2 us -> 53.4 us (0.985)
  Pallas kernels: 52.8 us -> 52 us
    pallas_call x1, Pallas kernels: 52.8 us -> 52 us  [local_build(): pl.pallas_call(kernel, out_shape=[pltpu.VMEM((2 * ROWS, 128), F32), pltpu...]
where the time goes in v5:
time: 53.4 us; the launch traced here: 53.3 us
  Pallas kernels  52 us (97%)
  between operations  0.64 us (1%)
  other arithmetic  0.63 us (1%)
    pallas_call x1, Pallas kernels, local_build(): pl.pallas_call(kernel, out_shape=[pltpu.VMEM((2 * ROWS, 128), F32), pltpu...  52 us

profile of v5, /device:TPU:3, one launch (start us, length us, event | category | flops | bytes accessed | tf_op | source)
XLA Modules:
  0.0 53.3 jit_solution(14322572561938268338)
XLA Ops:
  0.6 52.0 %shard_map.50 = (f32[128,128]{1,0:T(8,128)S(1)}, f32[64,128]{1,0:T(8,128)S(1)}) custom-call(f32[24576,256]{1,0:T(8,128)} %bitcast.3, f32[20,256]{1,0:T(8,128)} %bitcast.4, f32[19,256]{1,0:T(8,128)} %bitcast.5), custom_call_target="tpu_custom_call" | custom-call | tf_op jit(solution)/shard_map/pallas_call | solution.py:518
  52.7 0.6 %slice_subtract_fusion = (f32[64,128]{1,0:T(8,128)}, f32[64,128]{1,0:T(8,128)}) fusion(f32[64,128]{1,0:T(8,128)S(1)} %get-tuple-element.4, f32[128,128]{1,0:T(8,128)S(1)} %get-tuple-element.5), kind=kLoop, calls=%fused_computation | loop fusion | flops 16384 | bytes 163840 | tf_op jit(solution)/shard_map/sub | solution.py:549

commit v6 on v5

--- a/solution.py
+++ b/solution.py
@@ -24,6 +24,12 @@
 IA, I0, I1, I2, IT, I3, I4, I5 = 1, 1, 1, 1, 4, 4, 5, 6
 AHEAD = 4
 DEPTH = 6
+LANES = 128
+SIDE = 64
+PACK = 32
+ORBS = 40
+BODY = 16
+NT, NN, TN = ((1,), (1,)), ((1,), (0,)), ((0,), (0,))
 
 
 def dot(a, b, dims):
@@ -97,19 +103,19 @@
 
     ca_copy.wait()
     cb_copy.wait()
-    ct[0:16, :] = cav[0:16, :]
-    ct[16:32, :] = cbv[0:16, :]
-    ct[32:36, :] = cav[16:20, :]
-    ct[36:39, :] = cbv[16:19, :]
-    ct[39:40, :] = jnp.zeros((1, NB), F32)
+    ct[0:BODY, :] = cav[0:BODY, :]
+    ct[BODY:PACK, :] = cbv[0:BODY, :]
+    ct[PACK:36, :] = cav[BODY:20, :]
+    ct[36:39, :] = cbv[BODY:19, :]
+    ct[39:ORBS, :] = jnp.zeros((1, NB), F32)
     cs[...] = jnp.concatenate([t.astype(F32) for t in split(ct[...])], axis=0).astype(BF16)
-    own = ct[:, pl.ds(pl.multiple_of(x * 128, 128), 128)]
-    turned = pltpu.roll(own, 64, 1)
-    low = lax.broadcasted_iota(jnp.int32, (40, 128), 1) < 64
+    own = ct[:, pl.ds(pl.multiple_of(x * LANES, LANES), LANES)]
+    turned = pltpu.roll(own, SIDE, 1)
+    low = lax.broadcasted_iota(jnp.int32, (ORBS, LANES), 1) < SIDE
     own = jnp.where(low, jnp.where(c == 0, own, turned), jnp.where(c == 0, turned, own))
-    crep[:, :128] = own
-    crep[:, 128:] = own
-    sacc[96:128, :] = jnp.zeros((32, NB), F32)
+    crep[:, :LANES] = own
+    crep[:, LANES:] = own
+    sacc[96:LANES, :] = jnp.zeros((PACK, NB), F32)
 
     def part(spin, s, j, count=1):
         return tb.at[spin, s, pl.ds(pl.multiple_of(j * CROWS[spin], 8), count * CROWS[spin])]
@@ -120,21 +126,21 @@
         to_a = part(0, slot[kind], j)
         to_b = part(1, slot[kind], j)
         for h in range(CGROUPS // 2):
-            base = pl.multiple_of((first + 2 * h) * 256, 256)
+            base = pl.multiple_of((first + 2 * h) * NB, NB)
             b1, b2, b3 = split(bv[pl.ds(base, 512), :])
-            r1 = dot16(cs[...], b1, ((1,), (1,)))
-            r2 = dot16(cs[0:80, :], b2, ((1,), (1,)))
-            r3 = dot16(cs[0:40, :], b3, ((1,), (1,)))
-            r2 = ((r3 + r2[40:80] + r1[80:120]) + (r2[0:40] + r1[40:80])) + r1[0:40]
+            r1 = dot16(cs[...], b1, NT)
+            r2 = dot16(cs[0:80, :], b2, NT)
+            r3 = dot16(cs[0:ORBS, :], b3, NT)
+            r2 = ((r3 + r2[ORBS:80] + r1[80:120]) + (r2[0:ORBS] + r1[ORBS:80])) + r1[0:ORBS]
             for u in range(4):
                 p = 4 * h + u
-                r = r2[:, u * 128:(u + 1) * 128]
-                to_a[16 * p:16 * p + 16, :] = r[0:16]
-                to_b[16 * p:16 * p + 16, :] = r[16:32]
-                to_a[128 + 4 * p:132 + 4 * p, :] = r[32:36]
-                to_b[128 + 3 * p:131 + 3 * p, :] = r[36:39]
+                r = r2[:, u * LANES:(u + 1) * LANES]
+                to_a[BODY * p:BODY * p + BODY, :] = r[0:BODY]
+                to_b[BODY * p:BODY * p + BODY, :] = r[BODY:PACK]
+                to_a[LANES + 4 * p:132 + 4 * p, :] = r[PACK:36]
+                to_b[LANES + 3 * p:131 + 3 * p, :] = r[36:39]
             for u in range(2):
-                r = r2[:, u * 256:(u + 1) * 256]
+                r = r2[:, u * NB:(u + 1) * NB]
                 sacc[pl.ds(first + 2 * h + u, 1), :] = jnp.sum(r * crep[...], axis=0, keepdims=True)
 
     def remote_send(spin, kind, j, count=1):
@@ -225,7 +231,7 @@
     issue(I0)
 
     e8 = (lax.broadcasted_iota(jnp.int32, (8, NB), 1) // ROWS == lax.broadcasted_iota(jnp.int32, (8, NB), 0)).astype(F32)
-    gam[o] = dot(e8, sacc[...], ((1,), (1,)))
+    gam[o] = dot(e8, sacc[...], NT)
 
     def gamma_send(d):
         return pltpu.make_async_remote_copy(
@@ -246,12 +252,12 @@
         at = pl.ds(pl.multiple_of(j * CROWS[spin], 8), rows)
         a = tb[spin, s, at]
         b = tb[spin, s + 1, at]
-        left = lax.broadcasted_iota(jnp.int32, (rows, 128), 1) < 64
-        return jnp.where(left, a, pltpu.roll(b, 64, 1)), jnp.where(left, pltpu.roll(a, 64, 1), b)
+        left = lax.broadcasted_iota(jnp.int32, (rows, LANES), 1) < SIDE
+        return jnp.where(left, a, pltpu.roll(b, SIDE, 1)), jnp.where(left, pltpu.roll(a, SIDE, 1), b)
 
     for spin in range(2):
         cols = 2 * half * CROWS[spin]
-        acc = (jnp.zeros((128, 128), F32),) * 2
+        acc = (jnp.zeros((LANES, LANES), F32),) * 2
         for which in range(2):
             def dbody(h, acc):
                 for u in range(half):
@@ -259,15 +265,15 @@
                 m = jnp.concatenate(sides(spin, (4, 0)[which], h * half, half), axis=0)
                 m1, m2, m3 = split(m)
                 t1, t2, t3 = split(m.T)
-                r = dot16(jnp.concatenate([t1, t2], axis=0), jnp.concatenate([m1, m2], axis=1), ((1,), (0,)))
-                q = dot16(t1, m3, ((1,), (0,)))
+                r = dot16(jnp.concatenate([t1, t2], axis=0), jnp.concatenate([m1, m2], axis=1), NN)
+                q = dot16(t1, m3, NN)
                 if which == 1:
                     lt[spin, h, :, 0:cols] = jnp.concatenate([t1, t2, t3], axis=0)
-                return acc[0] + ((r[128:, 128:] + (r[:128, 128:] + r[128:, :128])) + r[:128, :128]), acc[1] + q
+                return acc[0] + ((r[LANES:, LANES:] + (r[:LANES, LANES:] + r[LANES:, :LANES])) + r[:LANES, :LANES]), acc[1] + q
             acc = lax.fori_loop(0, 2, dbody, acc)
         acc = acc[0] + (acc[1] + acc[1].T)
-        kd[spin, 0] = acc[:64]
-        kd[spin, 1] = acc[64:]
+        kd[spin, 0] = acc[:SIDE]
+        kd[spin, 1] = acc[SIDE:]
         if spin == 1:
             for u in range(half):
                 lc[u, :, 0:2 * CROWS[1]] = jnp.concatenate(split(jnp.concatenate(sides(1, 0, half + u, 1), axis=0).T), axis=0)
@@ -364,25 +370,25 @@
         rows = count * CROWS[spin]
         v = tb[spin, 2 + cs, j * CROWS[spin]:j * CROWS[spin] + rows]
         v1, v2, v3 = [t.astype(F32) for t in split(v)]
-        left = lax.broadcasted_iota(jnp.int32, (rows, 128), 1) < 64
-        none = jnp.zeros((rows, 128), F32)
+        left = lax.broadcasted_iota(jnp.int32, (rows, LANES), 1) < SIDE
+        none = jnp.zeros((rows, LANES), F32)
         w = jnp.concatenate([
-            jnp.concatenate([jnp.where(left, v1, pltpu.roll(v2, 64, 1)), jnp.where(left, v3, none)], axis=1),
-            jnp.concatenate([jnp.where(left, pltpu.roll(v1, 64, 1), v2), jnp.where(left, pltpu.roll(v3, 64, 1), none)], axis=1),
+            jnp.concatenate([jnp.where(left, v1, pltpu.roll(v2, SIDE, 1)), jnp.where(left, v3, none)], axis=1),
+            jnp.concatenate([jnp.where(left, pltpu.roll(v1, SIDE, 1), v2), jnp.where(left, pltpu.roll(v3, SIDE, 1), none)], axis=1),
         ], axis=0).astype(BF16)
-        r = dot16(left_side[:, 0:2 * rows], w, ((1,), (0,)))
-        return acc + ((r[256:] + r[128:256]) + r[:128])
+        r = dot16(left_side[:, 0:2 * rows], w, NN)
+        return acc + ((r[NB:] + r[LANES:NB]) + r[:LANES])
 
     def off_done(spin, cs, acc):
-        block = acc[:, :128] + acc[:, 128:]
-        block = block + pltpu.roll(block, 64, 1)
-        left = lax.broadcasted_iota(jnp.int32, (32, 128), 1) < 64
-        kt[spin, cs] = block.T[:64]
+        block = acc[:, :LANES] + acc[:, LANES:]
+        block = block + pltpu.roll(block, SIDE, 1)
+        left = lax.broadcasted_iota(jnp.int32, (PACK, LANES), 1) < SIDE
+        kt[spin, cs] = block.T[:SIDE]
         for cd in range(2):
-            kp[spin, cs, cd] = jnp.where(left, block[64 * cd:64 * cd + 32], pltpu.roll(block[64 * cd + 32:64 * cd + 64], 64, 1))
+            kp[spin, cs, cd] = jnp.where(left, block[SIDE * cd:SIDE * cd + PACK], pltpu.roll(block[SIDE * cd + PACK:SIDE * cd + SIDE], SIDE, 1))
         each_ko(spin, cs, start)
 
-    zero = jnp.zeros((128, NB), F32)
+    zero = jnp.zeros((LANES, NB), F32)
     for spin in range(2):
         acc = zero
         for h in range(2):
@@ -396,19 +402,19 @@
         gamma_recv(d).wait_recv()
     gsum = (gam[0] + gam[1]) + (gam[2] + gam[3])
     for k in range(GRP):
-        pick = (lax.broadcasted_iota(jnp.int32, (8, 128), 0) == k).astype(F32)
-        grep[k] = dot(gsum, pick, ((0,), (0,)))
+        pick = (lax.broadcasted_iota(jnp.int32, (8, LANES), 0) == k).astype(F32)
+        grep[k] = dot(gsum, pick, TN)
 
     def jbody(g, acc):
         for k in range(GRP):
             row = grep[k, pl.ds(g, 1), :]
-            base = pl.multiple_of(g * 256 + k * ROWS, ROWS)
+            base = pl.multiple_of(g * NB + k * ROWS, ROWS)
             acc = acc + bv[pl.ds(base, ROWS), :] * jnp.concatenate([row, row], axis=1)
         return acc
 
     jacc = lax.fori_loop(0, NQ // GRP, jbody, jnp.zeros((ROWS, NB), F32))
-    jp[0] = jacc[:, :128]
-    jp[1] = jacc[:, 128:]
+    jp[0] = jacc[:, :LANES]
+    jp[1] = jacc[:, LANES:]
     j_copy = pltpu.make_async_remote_copy(
         src_ref=jp.at[1 - y], dst_ref=jr, send_sem=j_s, recv_sem=j_r,
         device_id={'aux': 1 - y}, device_id_type=MESH)
@@ -429,7 +435,7 @@
             s = lax.rem(2 * y + c + d, 4)
             landed(gd.at[spin, s], gd_r.at[spin, s])
             total = total + gd[spin, s]
-        s_ref[spin * 64:spin * 64 + 64, :] = total
+        s_ref[spin * SIDE:spin * SIDE + SIDE, :] = total
 
     def finish_ko(spin):
         pair_sum = []
@@ -455,9 +461,9 @@
                 kr[1, 1] = (gt[0] + gt[1]) + (gt[2] + gt[3])
             turned = kr[1, 1]
         a, b = pair_sum
-        left = lax.broadcasted_iota(jnp.int32, (32, 128), 1) < 64
-        s_ref[spin * 64:spin * 64 + 32, :] = turned[:32] + jnp.where(left, a, pltpu.roll(b, 64, 1))
-        s_ref[spin * 64 + 32:spin * 64 + 64, :] = turned[32:] + jnp.where(left, pltpu.roll(a, 64, 1), b)
+        left = lax.broadcasted_iota(jnp.int32, (PACK, LANES), 1) < SIDE
+        s_ref[spin * SIDE:spin * SIDE + PACK, :] = turned[:PACK] + jnp.where(left, a, pltpu.roll(b, SIDE, 1))
+        s_ref[spin * SIDE + PACK:spin * SIDE + SIDE, :] = turned[PACK:] + jnp.where(left, pltpu.roll(a, SIDE, 1), b)
 
     acc = zero
     for j, count in ((0, half), (half, 1), (half + 1, 1), (half + 2, 1)):
@@ -517,24 +523,24 @@
         vmem = pltpu.VMEM
         neg, coul = pl.pallas_call(
             kernel,
-            out_shape=[pltpu.VMEM((2 * ROWS, 128), F32), pltpu.VMEM((ROWS, 128), F32)],
+            out_shape=[pltpu.VMEM((2 * ROWS, LANES), F32), pltpu.VMEM((ROWS, LANES), F32)],
             in_specs=[pl.BlockSpec(memory_space=pl.ANY)] * 3,
             out_specs=[pl.BlockSpec(memory_space=vmem)] * 2,
             scratch_shapes=[
                 vmem((NQ * ROWS, NB), F32),
-                vmem((2, 8, TROWS, 128), F32),
+                vmem((2, 8, TROWS, LANES), F32),
                 vmem((20, NB), F32), vmem((19, NB), F32),
-                vmem((40, NB), F32), vmem((120, NB), BF16), vmem((40, NB), F32),
-                vmem((128, NB), F32),
-                vmem((4, 8, 128), F32),
-                vmem((GRP, 128, 128), F32),
+                vmem((ORBS, NB), F32), vmem((120, NB), BF16), vmem((ORBS, NB), F32),
+                vmem((LANES, NB), F32),
+                vmem((4, 8, LANES), F32),
+                vmem((GRP, LANES, LANES), F32),
                 vmem((2, 2, 384, CHUNKS * CROWS[0]), BF16),
                 vmem((CHUNKS // 2, 384, 384), BF16),
-                vmem((2, 2, 64, 128), F32), vmem((2, 2, 2, 32, 128), F32), vmem((2, 2, 64, 128), F32),
-                vmem((2, 2, 64, 128), F32),
-                vmem((2, 4, 64, 128), F32), vmem((2, 2, 4, 32, 128), F32), vmem((4, 64, 128), F32),
-                vmem((2, 4, 64, 128), F32),
-                vmem((2, 64, 128), F32), vmem((64, 128), F32),
+                vmem((2, 2, SIDE, LANES), F32), vmem((2, 2, 2, PACK, LANES), F32), vmem((2, 2, SIDE, LANES), F32),
+                vmem((2, 2, SIDE, LANES), F32),
+                vmem((2, 4, SIDE, LANES), F32), vmem((2, 2, 4, PACK, LANES), F32), vmem((4, SIDE, LANES), F32),
+                vmem((2, 4, SIDE, LANES), F32),
+                vmem((2, SIDE, LANES), F32), vmem((SIDE, LANES), F32),
                 dma((4, CHUNKS)), dma((2,)),
                 dma((2, 2, CHUNKS)), dma((2, 2, CHUNKS)),
                 dma((2, 2, CHUNKS)), dma((2, 2, CHUNKS)),

time: 53.4 us -> 53.4 us (level)
  no operation moved by 1% of the time
where the time goes in v6:
time: 53.4 us; the launch traced here: 53.3 us
  Pallas kernels  52 us (97%)
  between operations  0.64 us (1%)
  other arithmetic  0.63 us (1%)
    pallas_call x1, Pallas kernels, local_build(): pl.pallas_call(kernel, out_shape=[pltpu.VMEM((2 * ROWS, LANES), F32), plt...  52 us

profile of v6, /device:TPU:3, one launch (start us, length us, event | category | flops | bytes accessed | tf_op | source)
XLA Modules:
  0.0 53.3 jit_solution(14322572561938268338)
XLA Ops:
  0.6 52.0 %shard_map.50 = (f32[128,128]{1,0:T(8,128)S(1)}, f32[64,128]{1,0:T(8,128)S(1)}) custom-call(f32[24576,256]{1,0:T(8,128)} %bitcast.3, f32[20,256]{1,0:T(8,128)} %bitcast.4, f32[19,256]{1,0:T(8,128)} %bitcast.5), custom_call_target="tpu_custom_call" | custom-call | tf_op jit(solution)/shard_map/pallas_call | solution.py:524
  52.7 0.6 %slice_subtract_fusion = (f32[64,128]{1,0:T(8,128)}, f32[64,128]{1,0:T(8,128)}) fusion(f32[64,128]{1,0:T(8,128)S(1)} %get-tuple-element.4, f32[128,128]{1,0:T(8,128)S(1)} %get-tuple-element.5), kind=kLoop, calls=%fused_computation | loop fusion | flops 16384 | bytes 163840 | tf_op jit(solution)/shard_map/sub | solution.py:555
